TPU v7x, 32 devices: a whole 2x2x4 slice. The times are simulated.
32 devices in a mesh: groups: 2 (over x), seq: 16 (over z, y, core).
Axes of the slice: x: 2, y: 2, z: 4, core: 2. Of those that a mesh axis runs over, the one named last changes fastest.
Arguments:
- queries: bfloat16 [4, 128, 8192], P(None, ('groups', 'seq')), parts along dimension 1, may hold values from -16 to 16
- new_keys: bfloat16 [4, 128, 1024], P(None, ('groups', 'seq')), parts along dimension 1, may hold values from -6 to 6
- new_values: bfloat16 [4, 128, 1024], P(None, ('groups', 'seq')), parts along dimension 1, may hold values from -6 to 6
- pool_keys: bfloat16 [2048, 16, 1024], P(('groups', 'seq')), parts along dimension 0, may hold values from -6 to 6
- pool_values: bfloat16 [2048, 16, 1024], P(('groups', 'seq')), parts along dimension 0, may hold values from -6 to 6
- page_table: int32 [128, 16], P(('groups', 'seq')), parts along dimension 0, may hold values from 0 to 63, as said below
- cached_len: int32 [128], P(('groups', 'seq')), parts along dimension 0, may hold values from 1 to 256
- turn_keys: bfloat16 [4, 32, 16, 1024], P(None, ('groups', 'seq')), parts along dimension 1, may hold values from -6 to 6
- turn_values: bfloat16 [4, 32, 16, 1024], P(None, ('groups', 'seq')), parts along dimension 1, may hold values from -6 to 6
- turn_lengths: int32 [32], P('groups'), parts along dimension 0, may hold values from 1 to 80, 768 in all
- turn_slot: int32 [32], P('groups'), parts along dimension 0, may hold values from 0 to 63, as said below
Outputs:
- attended: bfloat16 [4, 128, 8192], P(None, ('groups', 'seq')), parts along dimension 1
- landed_keys: bfloat16 [32, 80, 1024], P(('groups', 'seq')), parts along dimension 0
- landed_values: bfloat16 [32, 80, 1024], P(('groups', 'seq')), parts along dimension 0
There are 2 independent parts, one for each index of `groups`. A program takes and returns all parts, laid end to end along the dimension named above; each array names one. Nothing has to cross between parts.
Inputs may be any that keep to these rules, and one draw needn't show every extreme that they name: `page_table`: the 4 rows of each device's slots together hold every number of 0 to 63 exactly once. `turn_lengths`: they sum to 768; the largest is exactly 80. `turn_slot`: each block of 4 slots holds the slot of exactly one turn.
All inputs are finite; a program needn't handle non-finite values.
Results may differ from a plain program's by a relative error of at most 0.0049.
Values may be sent and summed in bfloat16 or wider, within the bound.
No kernel may reach another device: no remote copies, remote signals or barrier semaphores. Data moves between devices by JAX's collectives and lax.ppermute only.
A program may use at most 128 MiB of HBM per device.

v0:
```python
import functools
import math

import jax
import jax.numpy as jnp
from jax import lax
from jax.experimental import pallas as pl
from jax.experimental.pallas import tpu as pltpu
from jax.sharding import PartitionSpec as P


QH = 64
KVH = 8
HD = 128
MOSTT = 80


SHARE = QH // KVH
LOG2_SCALE = math.log2(math.e) / math.sqrt(HD)
VMEM = pl.BlockSpec(memory_space=pltpu.VMEM)
SMEM = pl.BlockSpec(memory_space=pltpu.SMEM)
HBM = pl.BlockSpec(memory_space=pltpu.HBM)
TRANSPOSED = (((1,), (1,)), ((), ()))


def turn_of(lengths, owners, page_rows, slots_here, owner):
    def look(t, carry):
        first, start, count, length, slot = carry
        tokens = lengths[t]
        pages = (tokens + page_rows - 1) // page_rows
        whose = owners[t]
        mine = whose // slots_here == owner
        return (
            first + pages,
            jnp.where(mine, first, start),
            jnp.where(mine, pages, count),
            jnp.where(mine, tokens, length),
            jnp.where(mine, whose % slots_here, slot),
        )

    zero = jnp.int32(0)
    return lax.fori_loop(0, lengths.shape[0], look, (zero, zero, zero, zero, zero))[1:]


def prepare_kernel(
    chain, masks, laps, ints,
    place, *refs,
):
    ints_hbm, refs = refs[:ints], refs[ints:]
    q_hbm, new_k_hbm, new_v_hbm, pool_k, pool_v = refs[:5]
    q_all, new_all, k_buf, v_buf, pick_mask, land_mask, bias, mine_mask = refs[5:13]
    q, new_k, new_v = refs[13:16]
    turn_lengths, turn_slot = refs[16 : 16 + ints]
    sems = refs[16 + ints]
    steps, slots, _ = q.shape
    page_rows = k_buf.shape[1]
    rows = steps * SHARE
    half = chain // 2
    pairs = (
        (ints_hbm[0], turn_lengths), (ints_hbm[1], turn_slot),
        (q_hbm, q), (new_k_hbm, new_k), (new_v_hbm, new_v), (pool_k, k_buf), (pool_v, v_buf),
    )
    copies = [pltpu.make_async_copy(*pair, sems.at[i]) for i, pair in enumerate(pairs)]
    for copy in copies:
        copy.start()
    for copy in copies[:2]:
        copy.wait()

    me = place[0]
    row = lax.broadcasted_iota(jnp.int32, (page_rows, HD), 0)
    for i, mask in enumerate(masks):
        start, count, _, _ = turn_of(turn_lengths, turn_slot, page_rows, slots, me ^ mask)
        for slot in range(2):
            residue = me ^ slot
            page = start + ((residue - start) & (half - 1))
            for side in range(2):
                for lap in range(laps):
                    wanted = lap * chain + (residue ^ (side * half))
                    hit = (page == wanted) & (page < start + count)
                    pick_mask[((i * 2 + slot) * 2 + side) * laps + lap] = jnp.full(
                        (page_rows, HD), hit.astype(jnp.float32)
                    ).astype(jnp.bfloat16)
    start, count, length, my_slot = turn_of(turn_lengths, turn_slot, page_rows, slots, me)
    for j in range(land_mask.shape[0]):
        kept = (row + j * page_rows < length).astype(jnp.float32)
        for i, mask in enumerate(masks):
            for slot in range(2):
                hit = (((me ^ mask ^ slot) - start) & (half - 1)) == j
                land_mask[j, i * 2 + slot] = (kept * hit.astype(jnp.float32)).astype(jnp.bfloat16)
    token = lax.broadcasted_iota(jnp.int32, bias.shape, 1)
    bias[...] = jnp.where(token < length, 0.0, -jnp.inf)
    mine_mask[...] = (
        lax.broadcasted_iota(jnp.int32, mine_mask.shape, 0) == my_slot
    ).astype(jnp.float32)

    for copy in copies[2:5]:
        copy.wait()
    for kv, new in enumerate((new_k, new_v)):
        for t in range(steps):
            for g in range(KVH):
                new_all[kv, pl.ds((t * KVH + g) * slots, slots), :] = new[
                    t, :, pl.ds(g * HD, HD)
                ].astype(jnp.float32)
    for s in range(steps):
        for g in range(KVH):
            for e in range(SHARE):
                tile = q[s, :, pl.ds((g * SHARE + e) * HD, HD)].astype(jnp.float32)
                q_all[pl.ds(g * rows + s * SHARE + e, slots, stride=KVH * rows), :] = tile
    for copy in copies[5:]:
        copy.wait()


def resident_kernel(
    place, turn_lengths_hbm, turn_slot_hbm, table_hbm, lengths_hbm, q_all, new_all, k_buf, v_buf,
    out, q_mine, acc_mine, max_mine, sum_mine,
    turn_lengths, turn_slot, table, lengths, s_new, p_new, acc_all, max_all, sum_all, sems,
):
    steps, slots, _ = out.shape
    page_rows = k_buf.shape[1]
    pages = table.shape[1]
    span = pages * page_rows
    rows = steps * SHARE
    pairs = (
        (turn_lengths_hbm, turn_lengths), (turn_slot_hbm, turn_slot),
        (table_hbm, table), (lengths_hbm, lengths),
    )
    copies = [pltpu.make_async_copy(*pair, sems.at[i]) for i, pair in enumerate(pairs)]
    for copy in copies:
        copy.start()

    fresh = (steps * KVH * slots, HD)
    block = KVH * rows
    column = lax.broadcasted_iota(jnp.int32, (block, fresh[0]), 1)
    head_row = lax.broadcasted_iota(jnp.int32, (block, fresh[0]), 0)
    column_slot = column % slots
    causal = (column // slots % KVH == head_row // rows) & (
        column // (slots * KVH) <= head_row % rows // SHARE
    )
    new_keys = new_all[0].astype(jnp.bfloat16)
    for r in range(slots):
        part = pl.ds(r * block, block)
        score = lax.dot_general(
            q_all[part, :].astype(jnp.bfloat16), new_keys, TRANSPOSED,
            preferred_element_type=jnp.float32,
        )
        s_new[part, :] = jnp.where(causal & (column_slot == r), score * LOG2_SCALE, -jnp.inf)

    token = lax.broadcasted_iota(jnp.int32, (2 * rows, span), 1)
    none = jnp.zeros((rows, HD), jnp.bfloat16)
    for copy in copies:
        copy.wait()
    my_slot = turn_of(turn_lengths, turn_slot, page_rows, slots, place[0])[3]
    for r in range(slots):
        valid = token < lengths[r]
        where = [table[r, c] for c in range(pages)]
        scores = []
        for g in range(0, KVH, 2):
            first = q_all[pl.ds(r * block + g * rows, rows), :].astype(jnp.bfloat16)
            second = q_all[pl.ds(r * block + (g + 1) * rows, rows), :].astype(jnp.bfloat16)
            both = jnp.concatenate(
                [jnp.concatenate([first, none], 1), jnp.concatenate([none, second], 1)]
            )
            keys = jnp.concatenate([k_buf[c, :, pl.ds(g * HD, 2 * HD)] for c in where])
            scores.append(
                lax.dot_general(both, keys, TRANSPOSED, preferred_element_type=jnp.float32)
            )
        for i, g in enumerate(range(0, KVH, 2)):
            part = pl.ds(r * block + g * rows, 2 * rows)
            score = jnp.where(valid, scores[i] * LOG2_SCALE, -jnp.inf)
            late = s_new[part, :]
            top = jnp.maximum(
                jnp.max(score, axis=1, keepdims=True), jnp.max(late, axis=1, keepdims=True)
            )
            prob = jnp.exp2(score - top)
            late = jnp.exp2(late - top)
            total = jnp.sum(prob, axis=1, keepdims=True) + jnp.sum(late, axis=1, keepdims=True)
            max_all[part, :] = jnp.broadcast_to(top, (2 * rows, HD))
            sum_all[part, :] = jnp.broadcast_to(total, (2 * rows, HD))
            p_new[part, :] = late.astype(jnp.bfloat16)
            values = jnp.concatenate([v_buf[c, :, pl.ds(g * HD, 2 * HD)] for c in where])
            acc = jnp.dot(prob.astype(jnp.bfloat16), values, preferred_element_type=jnp.float32)
            acc_all[pl.ds(r * block + g * rows, rows), :] = acc[:rows, :HD]
            acc_all[pl.ds(r * block + (g + 1) * rows, rows), :] = acc[rows:, HD:]
    new_values = new_all[1].astype(jnp.bfloat16)
    for r in range(slots):
        part = pl.ds(r * block, block)
        acc_all[part, :] += jnp.dot(
            p_new[part, :], new_values, preferred_element_type=jnp.float32
        )

    mine = pl.ds(pl.multiple_of(my_slot * block, block), block)
    acc_mine[...] = acc_all[mine, :]
    max_mine[...] = max_all[mine, :]
    sum_mine[...] = sum_all[mine, :]
    for g in range(0, KVH, 2):
        first = q_all[pl.ds(pl.multiple_of(my_slot * block + g * rows, rows), rows), :]
        second = q_all[pl.ds(pl.multiple_of(my_slot * block + (g + 1) * rows, rows), rows), :]
        q_mine[pl.ds(g * rows, rows), pl.ds(0, HD)] = first.astype(jnp.bfloat16)
        q_mine[pl.ds(g * rows, rows), pl.ds(HD, HD)] = none
        q_mine[pl.ds((g + 1) * rows, rows), pl.ds(0, HD)] = none
        q_mine[pl.ds((g + 1) * rows, rows), pl.ds(HD, HD)] = second.astype(jnp.bfloat16)
    acc_all[...] = acc_all[...] / sum_all[...]
    for s in range(steps):
        for g in range(KVH):
            for e in range(SHARE):
                tile = acc_all[pl.ds(g * rows + s * SHARE + e, slots, stride=block), :]
                out[s, :, pl.ds((g * SHARE + e) * HD, HD)] = tile.astype(jnp.bfloat16)


def pick_kernel(laps, pick_mask, own, twin, got, got_twin, *outs):
    width = own.shape[2]
    for i, out in enumerate(outs):
        for slot, sides in enumerate(((own, got), (twin, got_twin))):
            hits = [
                pick_mask[((i * 2 + slot) * 2 + side) * laps + lap] > 0
                for side in range(2)
                for lap in range(laps)
            ]
            for lane in range(0, width, HD):
                lanes = pl.ds(lane, HD)
                pages = [sides[side][lap, :, lanes] for side in range(2) for lap in range(laps)]
                best = jnp.zeros_like(pages[0])
                for hit, page in zip(hits, pages):
                    best = jnp.where(hit, page, best)
                out[slot, :, lanes] = best


def land_kernel(
    masks, part_out, q, acc_old, max_old, sum_old, land_mask, bias, mine_mask, *refs
):
    pieces = refs[: len(masks)], refs[len(masks) : 2 * len(masks)]
    out, landed_k, landed_v, o_new = refs[2 * len(masks) :]
    steps, _, _ = out.shape
    pages, _, page_rows, _ = land_mask.shape
    width = landed_k.shape[2]
    span = pages * page_rows
    rows = steps * SHARE
    for j in range(pages):
        hits = [land_mask[j, i] > 0 for i in range(2 * len(masks))]
        for kv, landed in enumerate((landed_k, landed_v)):
            for lane in range(0, width, HD):
                lanes = pl.ds(lane, HD)
                found = jnp.zeros((page_rows, HD), jnp.bfloat16)
                for i, hit in enumerate(hits):
                    found = jnp.where(hit, pieces[kv][i // 2][i % 2, :, lanes], found)
                landed[0, pl.ds(j * page_rows, page_rows), lanes] = found
    for g in range(0, KVH, 2):
        part = pl.ds(g * rows, 2 * rows)
        lanes = pl.ds(g * HD, 2 * HD)
        score = lax.dot_general(
            q[part, :], landed_k[0, :, lanes], TRANSPOSED, preferred_element_type=jnp.float32
        )
        score = score * LOG2_SCALE + bias[:, :span]
        before = max_old[part, :]
        top = jnp.maximum(before, jnp.max(score, axis=1, keepdims=True))
        prob = jnp.exp2(score - top[:, :span])
        shrink = jnp.exp2(before - top)
        total = sum_old[part, :] * shrink + jnp.sum(prob, axis=1, keepdims=True)
        acc = jnp.dot(
            prob.astype(jnp.bfloat16), landed_v[0, :, lanes], preferred_element_type=jnp.float32
        )
        acc = jnp.concatenate([acc[:rows, :HD], acc[rows:, HD:]])
        o_new[part, :] = (acc_old[part, :] * shrink + acc) / total
    mine = mine_mask[...] > 0
    for s in range(steps):
        for g in range(KVH):
            for e in range(SHARE):
                lanes = pl.ds((g * SHARE + e) * HD, HD)
                fresh = o_new[pl.ds(g * rows + s * SHARE + e, 1), :]
                tile = part_out[s, :, lanes].astype(jnp.float32)
                out[s, :, lanes] = jnp.where(mine, fresh, tile).astype(jnp.bfloat16)


def per_device(
    queries, new_keys, new_values, pool_keys, pool_values, page_table, cached_len,
    turn_keys, turn_values, turn_lengths, turn_slot,
):
    chain = lax.axis_size("seq")
    steps, slots, _ = queries.shape
    page_rows, width = pool_keys.shape[1:]
    pages = page_table.shape[1]
    laps = turn_keys.shape[0]
    most_pages = -(-MOSTT // page_rows)
    half = chain // 2
    assert chain & (chain - 1) == 0 and most_pages <= half
    masks = tuple(range(0, half, 2))
    rows = steps * SHARE

    def swap(x, mask):
        return lax.ppermute(x, "seq", [(i, i ^ mask) for i in range(chain)])

    def kernel(body, **settings):
        def call(*args):
            return pl.pallas_call(body, **settings)(*args)

        return call

    place = lax.axis_index("seq").reshape(1).astype(jnp.int32)

    f32, bf16 = jnp.float32, jnp.bfloat16
    block = KVH * rows
    stats = jax.ShapeDtypeStruct((block, HD), f32)
    all_rows = pltpu.VMEM((slots * block, HD), f32)
    fresh = (steps * KVH * slots, HD)
    own_k = turn_keys.reshape(laps, page_rows, width)
    own_v = turn_values.reshape(laps, page_rows, width)

    def in_hbm(*arrays):
        return tuple(pltpu.with_memory_space_constraint(x, pltpu.HBM) for x in arrays)

    got_k = swap(own_k, half)
    twin_k, twin_v = swap(own_k, 1), swap(own_v, 1)
    large = in_hbm(queries, new_keys, new_values, pool_keys, pool_values)
    ints = in_hbm(turn_lengths, turn_slot)
    more_ints = in_hbm(page_table, cached_len)
    q_all, new_all, k_buf, v_buf, pick_mask, land_mask, bias, mine_mask = kernel(
        functools.partial(prepare_kernel, chain, masks, laps, len(ints)),
        out_shape=(
            jax.ShapeDtypeStruct((slots * block, HD), f32),
            jax.ShapeDtypeStruct((2, *fresh), f32),
            jax.ShapeDtypeStruct(pool_keys.shape, bf16),
            jax.ShapeDtypeStruct(pool_values.shape, bf16),
            jax.ShapeDtypeStruct((len(masks) * 4 * laps, page_rows, HD), bf16),
            jax.ShapeDtypeStruct((most_pages, 2 * len(masks), page_rows, HD), bf16),
            jax.ShapeDtypeStruct((2 * rows, HD), f32),
            jax.ShapeDtypeStruct((slots, HD), f32),
        ),
        in_specs=[SMEM] + [HBM] * 7,
        out_specs=(VMEM,) * 8,
        scratch_shapes=[
            *(pltpu.VMEM(x.shape, bf16) for x in large[:3]),
            *(pltpu.SMEM(x.shape, jnp.int32) for x in ints),
            pltpu.SemaphoreType.DMA((7,)),
        ],
        compiler_params=pltpu.CompilerParams(vmem_limit_bytes=16 * 2**20),
    )(place, *ints, *large)
    own_v, q_all = lax.optimization_barrier((own_v, q_all))
    got_v = swap(own_v, half)
    part_out, q_mine, acc, top, total = kernel(
        resident_kernel,
        out_shape=(
            jax.ShapeDtypeStruct(queries.shape, bf16),
            jax.ShapeDtypeStruct((block, 2 * HD), bf16),
            stats, stats, stats,
        ),
        in_specs=[SMEM] + [HBM] * 4 + [VMEM] * 4,
        out_specs=(VMEM,) * 5,
        scratch_shapes=[
            *(pltpu.SMEM(x.shape, jnp.int32) for x in ints + more_ints),
            all_rows,
            pltpu.VMEM((slots * block, HD), bf16),
            all_rows, all_rows, all_rows,
            pltpu.SemaphoreType.DMA((4,)),
        ],
        compiler_params=pltpu.CompilerParams(vmem_limit_bytes=16 * 2**20),
        cost_estimate=pl.CostEstimate(
            flops=4 * slots * block * pages * page_rows * HD,
            bytes_accessed=2 * pool_keys.size * 2, transcendentals=0,
        ),
    )(place, *ints, *more_ints, q_all, new_all, k_buf, v_buf)

    piece = jax.ShapeDtypeStruct((2, page_rows, width), bf16)

    def spread(own, twin, got):
        picked = kernel(
            functools.partial(pick_kernel, laps),
            out_shape=(piece,) * len(masks),
            in_specs=[VMEM] * 5,
            out_specs=(VMEM,) * len(masks),
            compiler_params=pltpu.CompilerParams(vmem_limit_bytes=8 * 2**20),
        )(pick_mask, own, twin, got, swap(got, 1))
        return [picked[0]] + [swap(x, mask) for x, mask in zip(picked[1:], masks[1:])]

    got_k, part_out = lax.optimization_barrier((got_k, part_out))
    pieces_k = spread(own_k, twin_k, got_k)
    pieces_v = spread(own_v, twin_v, got_v)

    landed = jax.ShapeDtypeStruct((1, most_pages * page_rows, width), bf16)
    return kernel(
        functools.partial(land_kernel, masks),
        out_shape=(jax.ShapeDtypeStruct(queries.shape, bf16), landed, landed),
        in_specs=[VMEM] * (8 + 2 * len(masks)),
        out_specs=(VMEM,) * 3,
        scratch_shapes=[pltpu.VMEM((block, HD), f32)],
        compiler_params=pltpu.CompilerParams(vmem_limit_bytes=8 * 2**20),
    )(part_out, q_mine, acc, top, total, land_mask, bias, mine_mask, *pieces_k, *pieces_v)


def solution(mesh):
    both = ("groups", "seq")
    in_specs = (
        P(None, both, None),
        P(None, both, None),
        P(None, both, None),
        P(both, None, None),
        P(both, None, None),
        P(both, None),
        P(both),
        P(None, both, None, None),
        P(None, both, None, None),
        P("groups"),
        P("groups"),
    )
    out_specs = (P(None, both, None), P(both, None, None), P(both, None, None))
    return jax.shard_map(
        per_device, mesh=mesh, in_specs=in_specs, out_specs=out_specs, check_vma=False
    )
```

profile of v0, /device:TPU:0, one launch (start us, length us, event | category | flops | bytes accessed | tf_op | source)
XLA Modules:
  0.0 30.0 jit_solution(5379101555433721821)
XLA Ops:
  0.6 4.1 %collective-permute-start = (bf16[4,16,1024]{2,1,0:T(8,128)(2,1)}, bf16[4,16,1024]{2,1,0:T(8,128)(2,1)S(1)}, u32[]{:S(2)}, u32[]{:S(2)}) collective-permute-start(bf16[4,16,1024]{2,1,0:T(8,128)(2,1)} %bitcast.3), channel_id=1, source_target_pairs={{0,8},{1,9},{2,10},{3,11},{4,12},{5,13},{6,14},{7,15},{8,0},{9,1},... | collective-permute-start | bytes 393224 | tf_op jit(solution)/shard_map/ppermute | solution.py:290
  4.8 2.7 %shard_map.130 = (f32[1024,128]{1,0:T(8,128)S(1)}, f32[2,128,128]{2,1,0:T(8,128)S(1)}, bf16[64,16,1024]{2,1,0:T(8,128)(2,1)S(1)}, bf16[64,16,1024]{2,1,0:T(8,128...) custom-call(s32[1]{0:T(128)} %bitcast.1.place, ...), custom_call_target="tpu_custom_call" | custom-call | tf_op jit(solution)/shard_map/pallas_call | solution.py:294
  7.5 0.1 collective-permute-start.7
  7.6 0.1 collective-permute-start.1
  7.7 3.1 %shard_map.131 = (bf16[4,4,8192]{2,1,0:T(4,128)(2,1)S(1)}, bf16[256,256]{1,0:T(8,128)(2,1)S(1)}, f32[256,128]{1,0:T(8,128)S(1)}, f32[256,128]{1,0:T(8,128)S(1)}, f32[256,128]{1,0:T(8,128)S(1)}) custom-call(s32[1]{0:T(128)} %bitcast.1.place, s32[16]{0:T(128)} %turn_lengths_hbm.1, s32[16]{0:T(128)} %turn_slot_hbm.1, s32[4,16]{1,0:T(4,128)} %table_hbm.1, ...), custom_call_target="tpu_custom_call" | custom-call | flops 134217728 | bytes 4194304 | tf_op jit(solution)/shard_map/pallas_call | solution.py:294
  10.7 4.0 %collective-permute-done.got = bf16[4,16,1024]{2,1,0:T(8,128)(2,1)S(1)} collective-permute-done((bf16[4,16,1024]{2,1,0:T(8,128)(2,1)}, bf16[4,16,1024]{2,1,0:T(8,128)(2,1)S(1)}, u32[]{:S(2)}, u32[]{:S(2)}) %collective-permute-start) | collective-permute-done | bytes 131104 | tf_op jit(solution)/shard_map/ppermute | solution.py:290
  14.8 0.0 collective-permute-start.2
  14.8 0.5 %collective-permute-start.6 = (bf16[4,16,1024]{2,1,0:T(8,128)(2,1)S(1)}, bf16[4,16,1024]{2,1,0:T(8,128)(2,1)S(1)}, u32[]{:S(2)}, u32[]{:S(2)}) collective-permute-start(bf16[4,16,1024]{2,1,0:T(8,128)(2,1)S(1)} %bitcast.7), channel_id=1, source_target_pairs={{0,1},{1,0},{2,3},{3,2},{4,5},{5,4},{6,7},{7,6},{8,9},{9,8},{10,11... | collective-permute-start | bytes 393224 | tf_op jit(solution)/shard_map/ppermute | solution.py:290
  15.3 1.6 %collective-permute-done.7.got = bf16[4,16,1024]{2,1,0:T(8,128)(2,1)S(1)} collective-permute-done((bf16[4,16,1024]{2,1,0:T(8,128)(2,1)S(1)}, bf16[4,16,1024]{2,1,0:T(8,128)(2,1)S(1)}, u32[]{:S(2)}, u32[]{:S(2)}) %collective-permute-start.7) | collective-permute-done | bytes 131104 | tf_op jit(solution)/shard_map/ppermute | solution.py:290
  16.9 0.0 collective-permute-start.8
  16.9 0.3 shard_map.132
  17.2 1.6 %collective-permute-start.3 = (bf16[2,16,1024]{2,1,0:T(8,128)(2,1)S(1)}, bf16[2,16,1024]{2,1,0:T(8,128)(2,1)S(1)}, u32[]{:S(2)}, u32[]{:S(2)}) collective-permute-start(bf16[2,16,1024]{2,1,0:T(8,128)(2,1)S(1)} %get-tuple-element.45), channel_id=1, source_target_pairs={{0,2},{1,3},{2,0},{3,1},{4,6},{5,7},{6,4},{7,5},{8,10},{9,11},{10,... | collective-permute-start | bytes 196616 | tf_op jit(solution)/shard_map/ppermute | solution.py:290
  18.8 0.7 %collective-permute-start.4 = (bf16[2,16,1024]{2,1,0:T(8,128)(2,1)S(1)}, bf16[2,16,1024]{2,1,0:T(8,128)(2,1)S(1)}, u32[]{:S(2)}, u32[]{:S(2)}) collective-permute-start(bf16[2,16,1024]{2,1,0:T(8,128)(2,1)S(1)} %get-tuple-element.46), channel_id=1, source_target_pairs={{0,4},{1,5},{2,6},{3,7},{4,0},{5,1},{6,2},{7,3},{8,12},{9,13},{10,... | collective-permute-start | bytes 196616 | tf_op jit(solution)/shard_map/ppermute | solution.py:290
  19.5 1.2 %collective-permute-start.5 = (bf16[2,16,1024]{2,1,0:T(8,128)(2,1)S(1)}, bf16[2,16,1024]{2,1,0:T(8,128)(2,1)S(1)}, u32[]{:S(2)}, u32[]{:S(2)}) collective-permute-start(bf16[2,16,1024]{2,1,0:T(8,128)(2,1)S(1)} %get-tuple-element.47), channel_id=1, source_target_pairs={{0,6},{1,7},{2,4},{3,5},{4,2},{5,3},{6,0},{7,1},{8,14},{9,15},{10,... | collective-permute-start | bytes 196616 | tf_op jit(solution)/shard_map/ppermute | solution.py:290
  20.7 0.3 shard_map.133
  21.0 0.8 %collective-permute-start.10 = (bf16[2,16,1024]{2,1,0:T(8,128)(2,1)S(1)}, bf16[2,16,1024]{2,1,0:T(8,128)(2,1)S(1)}, u32[]{:S(2)}, u32[]{:S(2)}) collective-permute-start(bf16[2,16,1024]{2,1,0:T(8,128)(2,1)S(1)} %get-tuple-element.51), channel_id=1, source_target_pairs={{0,4},{1,5},{2,6},{3,7},{4,0},{5,1},{6,2},{7,3},{8,12},{9,13},{10,... | collective-permute-start | bytes 196616 | tf_op jit(solution)/shard_map/ppermute | solution.py:290
  21.8 2.3 %collective-permute-start.11 = (bf16[2,16,1024]{2,1,0:T(8,128)(2,1)S(1)}, bf16[2,16,1024]{2,1,0:T(8,128)(2,1)S(1)}, u32[]{:S(2)}, u32[]{:S(2)}) collective-permute-start(bf16[2,16,1024]{2,1,0:T(8,128)(2,1)S(1)} %get-tuple-element.52), channel_id=1, source_target_pairs={{0,6},{1,7},{2,4},{3,5},{4,2},{5,3},{6,0},{7,1},{8,14},{9,15},{10,... | collective-permute-start | bytes 196616 | tf_op jit(solution)/shard_map/ppermute | solution.py:290
  24.1 0.0 collective-permute-done.3.refs_1_
  24.1 0.5 %collective-permute-start.9 = (bf16[2,16,1024]{2,1,0:T(8,128)(2,1)S(1)}, bf16[2,16,1024]{2,1,0:T(8,128)(2,1)S(1)}, u32[]{:S(2)}, u32[]{:S(2)}) collective-permute-start(bf16[2,16,1024]{2,1,0:T(8,128)(2,1)S(1)} %get-tuple-element.50), channel_id=1, source_target_pairs={{0,2},{1,3},{2,0},{3,1},{4,6},{5,7},{6,4},{7,5},{8,10},{9,11},{10,... | collective-permute-start | bytes 196616 | tf_op jit(solution)/shard_map/ppermute | solution.py:290
  24.6 0.4 %collective-permute-done.5.refs_3_ = bf16[2,16,1024]{2,1,0:T(8,128)(2,1)S(1)} collective-permute-done((bf16[2,16,1024]{2,1,0:T(8,128)(2,1)S(1)}, bf16[2,16,1024]{2,1,0:T(8,128)(2,1)S(1)}, u32[]{:S(2)}, u32[]{:S(2)}) %collective-permute-start.5) | collective-permute-done | bytes 65568 | tf_op jit(solution)/shard_map/ppermute | solution.py:290
  25.0 1.6 %collective-permute-done.10.refs_6_ = bf16[2,16,1024]{2,1,0:T(8,128)(2,1)S(1)} collective-permute-done((bf16[2,16,1024]{2,1,0:T(8,128)(2,1)S(1)}, bf16[2,16,1024]{2,1,0:T(8,128)(2,1)S(1)}, u32[]{:S(2)}, u32[]{:S(2)}) %collective-permute-start.10) | collective-permute-done | bytes 65568 | tf_op jit(solution)/shard_map/ppermute | solution.py:290
  26.5 1.0 %collective-permute-done.11.refs_7_ = bf16[2,16,1024]{2,1,0:T(8,128)(2,1)S(1)} collective-permute-done((bf16[2,16,1024]{2,1,0:T(8,128)(2,1)S(1)}, bf16[2,16,1024]{2,1,0:T(8,128)(2,1)S(1)}, u32[]{:S(2)}, u32[]{:S(2)}) %collective-permute-start.11) | collective-permute-done | bytes 65568 | tf_op jit(solution)/shard_map/ppermute | solution.py:290
  27.6 0.8 %collective-permute-done.9.refs_5_ = bf16[2,16,1024]{2,1,0:T(8,128)(2,1)S(1)} collective-permute-done((bf16[2,16,1024]{2,1,0:T(8,128)(2,1)S(1)}, bf16[2,16,1024]{2,1,0:T(8,128)(2,1)S(1)}, u32[]{:S(2)}, u32[]{:S(2)}) %collective-permute-start.9) | collective-permute-done | bytes 65568 | tf_op jit(solution)/shard_map/ppermute | solution.py:290
  28.4 1.6 %shard_map.134 = (bf16[4,4,8192]{2,1,0:T(4,128)(2,1)}, bf16[1,80,1024]{2,1,0:T(8,128)(2,1)}, bf16[1,80,1024]{2,1,0:T(8,128)(2,1)}) custom-call(bf16[4,4,8192]{2,1,0:T(4,128)(2,1)S(1)} %get-tuple-element.34.part_out, bf16[256,256]{1,0:T(8,128)(2,1)S(1)} %get-tuple-element.35.q, f32[256,128]{1,0:T(8,128)S(1)} %get-tuple-element.36.acc_old, ...), custom_call_target="tpu_custom_call" | custom-call | tf_op jit(solution)/shard_map/pallas_call | solution.py:294
  (9 shorter events, 0.0 us)
Async XLA Ops:
  0.6 14.1 %collective-permute-start = (bf16[4,16,1024]{2,1,0:T(8,128)(2,1)}, bf16[4,16,1024]{2,1,0:T(8,128)(2,1)S(1)}, u32[]{:S(2)}, u32[]{:S(2)}) collective-permute-start(bf16[4,16,1024]{2,1,0:T(8,128)(2,1)} %bitcast.3), channel_id=1, source_target_pairs={{0,8},{1,9},{2,10},{3,11},{4,12},{5,13},{6,14},{7,15},{8,0},{9,1},... | collective-permute-start | bytes 393224 | tf_op jit(solution)/shard_map/ppermute | solution.py:290
  4.8 2.7 %copy-start.1 = (bf16[4,1,16,1024]{3,2,1,0:T(8,128)(2,1)S(1)}, bf16[4,1,16,1024]{3,2,1,0:T(8,128)(2,1)}, u32[]{:S(2)}) copy-start(bf16[4,1,16,1024]{3,2,1,0:T(8,128)(2,1)} %param.19) | copy-start | bytes 393220
  4.8 2.8 %copy-start = (bf16[4,1,16,1024]{3,2,1,0:T(8,128)(2,1)S(1)}, bf16[4,1,16,1024]{3,2,1,0:T(8,128)(2,1)}, u32[]{:S(2)}) copy-start(bf16[4,1,16,1024]{3,2,1,0:T(8,128)(2,1)} %param.18) | copy-start | bytes 393220
  7.5 9.4 %collective-permute-start.7 = (bf16[4,16,1024]{2,1,0:T(8,128)(2,1)S(1)}, bf16[4,16,1024]{2,1,0:T(8,128)(2,1)S(1)}, u32[]{:S(2)}, u32[]{:S(2)}) collective-permute-start(bf16[4,16,1024]{2,1,0:T(8,128)(2,1)S(1)} %bitcast.6), channel_id=1, source_target_pairs={{0,8},{1,9},{2,10},{3,11},{4,12},{5,13},{6,14},{7,15},{8,0},{9,1},... | collective-permute-start | bytes 393224 | tf_op jit(solution)/shard_map/ppermute | solution.py:290
  7.6 9.3 %collective-permute-start.1 = (bf16[4,16,1024]{2,1,0:T(8,128)(2,1)S(1)}, bf16[4,16,1024]{2,1,0:T(8,128)(2,1)S(1)}, u32[]{:S(2)}, u32[]{:S(2)}) collective-permute-start(bf16[4,16,1024]{2,1,0:T(8,128)(2,1)S(1)} %bitcast.4), channel_id=1, source_target_pairs={{0,1},{1,0},{2,3},{3,2},{4,5},{5,4},{6,7},{7,6},{8,9},{9,8},{10,11... | collective-permute-start | bytes 393224 | tf_op jit(solution)/shard_map/ppermute | solution.py:290
  14.8 2.1 %collective-permute-start.2 = (bf16[4,16,1024]{2,1,0:T(8,128)(2,1)S(1)}, bf16[4,16,1024]{2,1,0:T(8,128)(2,1)S(1)}, u32[]{:S(2)}, u32[]{:S(2)}) collective-permute-start(bf16[4,16,1024]{2,1,0:T(8,128)(2,1)S(1)} %collective-permute-done.got), channel_id=1, source_target_pairs={{0,1},{1,0},{2,3},{3,2},{4,5},{5,4},{6,7},{7,6},{8,9},{9,8},{10,11... | collective-permute-start | bytes 393224 | tf_op jit(solution)/shard_map/ppermute | solution.py:290
  14.8 6.0 %collective-permute-start.6 = (bf16[4,16,1024]{2,1,0:T(8,128)(2,1)S(1)}, bf16[4,16,1024]{2,1,0:T(8,128)(2,1)S(1)}, u32[]{:S(2)}, u32[]{:S(2)}) collective-permute-start(bf16[4,16,1024]{2,1,0:T(8,128)(2,1)S(1)} %bitcast.7), channel_id=1, source_target_pairs={{0,1},{1,0},{2,3},{3,2},{4,5},{5,4},{6,7},{7,6},{8,9},{9,8},{10,11... | collective-permute-start | bytes 393224 | tf_op jit(solution)/shard_map/ppermute | solution.py:290
  16.9 3.8 %collective-permute-start.8 = (bf16[4,16,1024]{2,1,0:T(8,128)(2,1)S(1)}, bf16[4,16,1024]{2,1,0:T(8,128)(2,1)S(1)}, u32[]{:S(2)}, u32[]{:S(2)}) collective-permute-start(bf16[4,16,1024]{2,1,0:T(8,128)(2,1)S(1)} %collective-permute-done.7.got), channel_id=1, source_target_pairs={{0,1},{1,0},{2,3},{3,2},{4,5},{5,4},{6,7},{7,6},{8,9},{9,8},{10,11... | collective-permute-start | bytes 393224 | tf_op jit(solution)/shard_map/ppermute | solution.py:290
  17.2 6.9 %collective-permute-start.3 = (bf16[2,16,1024]{2,1,0:T(8,128)(2,1)S(1)}, bf16[2,16,1024]{2,1,0:T(8,128)(2,1)S(1)}, u32[]{:S(2)}, u32[]{:S(2)}) collective-permute-start(bf16[2,16,1024]{2,1,0:T(8,128)(2,1)S(1)} %get-tuple-element.45), channel_id=1, source_target_pairs={{0,2},{1,3},{2,0},{3,1},{4,6},{5,7},{6,4},{7,5},{8,10},{9,11},{10,... | collective-permute-start | bytes 196616 | tf_op jit(solution)/shard_map/ppermute | solution.py:290
  18.8 5.8 %collective-permute-start.4 = (bf16[2,16,1024]{2,1,0:T(8,128)(2,1)S(1)}, bf16[2,16,1024]{2,1,0:T(8,128)(2,1)S(1)}, u32[]{:S(2)}, u32[]{:S(2)}) collective-permute-start(bf16[2,16,1024]{2,1,0:T(8,128)(2,1)S(1)} %get-tuple-element.46), channel_id=1, source_target_pairs={{0,4},{1,5},{2,6},{3,7},{4,0},{5,1},{6,2},{7,3},{8,12},{9,13},{10,... | collective-permute-start | bytes 196616 | tf_op jit(solution)/shard_map/ppermute | solution.py:290
  19.5 5.5 %collective-permute-start.5 = (bf16[2,16,1024]{2,1,0:T(8,128)(2,1)S(1)}, bf16[2,16,1024]{2,1,0:T(8,128)(2,1)S(1)}, u32[]{:S(2)}, u32[]{:S(2)}) collective-permute-start(bf16[2,16,1024]{2,1,0:T(8,128)(2,1)S(1)} %get-tuple-element.47), channel_id=1, source_target_pairs={{0,6},{1,7},{2,4},{3,5},{4,2},{5,3},{6,0},{7,1},{8,14},{9,15},{10,... | collective-permute-start | bytes 196616 | tf_op jit(solution)/shard_map/ppermute | solution.py:290
  21.0 5.5 %collective-permute-start.10 = (bf16[2,16,1024]{2,1,0:T(8,128)(2,1)S(1)}, bf16[2,16,1024]{2,1,0:T(8,128)(2,1)S(1)}, u32[]{:S(2)}, u32[]{:S(2)}) collective-permute-start(bf16[2,16,1024]{2,1,0:T(8,128)(2,1)S(1)} %get-tuple-element.51), channel_id=1, source_target_pairs={{0,4},{1,5},{2,6},{3,7},{4,0},{5,1},{6,2},{7,3},{8,12},{9,13},{10,... | collective-permute-start | bytes 196616 | tf_op jit(solution)/shard_map/ppermute | solution.py:290
  21.8 5.8 %collective-permute-start.11 = (bf16[2,16,1024]{2,1,0:T(8,128)(2,1)S(1)}, bf16[2,16,1024]{2,1,0:T(8,128)(2,1)S(1)}, u32[]{:S(2)}, u32[]{:S(2)}) collective-permute-start(bf16[2,16,1024]{2,1,0:T(8,128)(2,1)S(1)} %get-tuple-element.52), channel_id=1, source_target_pairs={{0,6},{1,7},{2,4},{3,5},{4,2},{5,3},{6,0},{7,1},{8,14},{9,15},{10,... | collective-permute-start | bytes 196616 | tf_op jit(solution)/shard_map/ppermute | solution.py:290
  24.1 4.3 %collective-permute-start.9 = (bf16[2,16,1024]{2,1,0:T(8,128)(2,1)S(1)}, bf16[2,16,1024]{2,1,0:T(8,128)(2,1)S(1)}, u32[]{:S(2)}, u32[]{:S(2)}) collective-permute-start(bf16[2,16,1024]{2,1,0:T(8,128)(2,1)S(1)} %get-tuple-element.50), channel_id=1, source_target_pairs={{0,2},{1,3},{2,0},{3,1},{4,6},{5,7},{6,4},{7,5},{8,10},{9,11},{10,... | collective-permute-start | bytes 196616 | tf_op jit(solution)/shard_map/ppermute | solution.py:290
where the time goes:
time: 30.1 us; the launch traced here: 30 us
  starting transfers between devices  11.9 us (40%)
  waiting for transfers between devices  9.46 us (31%)
  Pallas kernels  7.89 us (26%)
  between operations  0.69 us (2%)
    ppermute x12, starting transfers between devices, swap(): return lax.ppermute(x, 'seq', [(i, i ^ mask) for i in range(chain)])  11.9 us
    ppermute x12, waiting for transfers between devices, swap(): return lax.ppermute(x, 'seq', [(i, i ^ mask) for i in range(chain)])  9.46 us
    pallas_call x5, Pallas kernels, call(): return pl.pallas_call(body, **settings)(*args)  7.89 us
  transfers between devices with their start and end apart: 12, of which 6 were waited for; matrix products, arithmetic and copies ran while one was open for 0% of the time, Pallas kernels for 21%

commit v1 on v0

--- a/solution.py
+++ b/solution.py
@@ -225,30 +225,29 @@
                 out[slot, :, lanes] = best
 
 
-def land_kernel(
-    masks, part_out, q, acc_old, max_old, sum_old, land_mask, bias, mine_mask, *refs
-):
-    pieces = refs[: len(masks)], refs[len(masks) : 2 * len(masks)]
-    out, landed_k, landed_v, o_new = refs[2 * len(masks) :]
-    steps, _, _ = out.shape
+def place_pages(land_mask, pieces, landed):
     pages, _, page_rows, _ = land_mask.shape
-    width = landed_k.shape[2]
-    span = pages * page_rows
-    rows = steps * SHARE
     for j in range(pages):
-        hits = [land_mask[j, i] > 0 for i in range(2 * len(masks))]
-        for kv, landed in enumerate((landed_k, landed_v)):
-            for lane in range(0, width, HD):
-                lanes = pl.ds(lane, HD)
-                found = jnp.zeros((page_rows, HD), jnp.bfloat16)
-                for i, hit in enumerate(hits):
-                    found = jnp.where(hit, pieces[kv][i // 2][i % 2, :, lanes], found)
-                landed[0, pl.ds(j * page_rows, page_rows), lanes] = found
+        hits = [land_mask[j, i] > 0 for i in range(2 * len(pieces))]
+        for lane in range(0, landed.shape[1], HD):
+            lanes = pl.ds(lane, HD)
+            found = jnp.zeros((page_rows, HD), jnp.bfloat16)
+            for i, hit in enumerate(hits):
+                found = jnp.where(hit, pieces[i // 2][i % 2, :, lanes], found)
+            landed[pl.ds(j * page_rows, page_rows), lanes] = found
+
+
+def land_keys_kernel(masks, q, acc_old, max_old, sum_old, land_mask, bias, *refs):
+    pieces = refs[: len(masks)]
+    landed, weights, base = refs[len(masks) :]
+    place_pages(land_mask, pieces, landed)
+    rows = q.shape[0] // KVH
+    span = landed.shape[0]
     for g in range(0, KVH, 2):
         part = pl.ds(g * rows, 2 * rows)
-        lanes = pl.ds(g * HD, 2 * HD)
         score = lax.dot_general(
-            q[part, :], landed_k[0, :, lanes], TRANSPOSED, preferred_element_type=jnp.float32
+            q[part, :], landed[:, pl.ds(g * HD, 2 * HD)], TRANSPOSED,
+            preferred_element_type=jnp.float32,
         )
         score = score * LOG2_SCALE + bias[:, :span]
         before = max_old[part, :]
@@ -256,11 +255,26 @@
         prob = jnp.exp2(score - top[:, :span])
         shrink = jnp.exp2(before - top)
         total = sum_old[part, :] * shrink + jnp.sum(prob, axis=1, keepdims=True)
+        weights[part, :] = (prob / total[:, :span]).astype(jnp.bfloat16)
+        base[part, :] = acc_old[part, :] * shrink / total
+
+
+def land_values_kernel(masks, part_out, weights, base, land_mask, mine_mask, *refs):
+    pieces = refs[: len(masks)]
+    out_hbm, landed_hbm, out, landed, o_new, sems = refs[len(masks) :]
+    steps = out.shape[0]
+    rows = steps * SHARE
+    place_pages(land_mask, pieces, landed)
+    copies = [pltpu.make_async_copy(landed, landed_hbm, sems.at[steps])]
+    copies[0].start()
+    for g in range(0, KVH, 2):
         acc = jnp.dot(
-            prob.astype(jnp.bfloat16), landed_v[0, :, lanes], preferred_element_type=jnp.float32
+            weights[pl.ds(g * rows, 2 * rows), :], landed[:, pl.ds(g * HD, 2 * HD)],
+            preferred_element_type=jnp.float32,
         )
-        acc = jnp.concatenate([acc[:rows, :HD], acc[rows:, HD:]])
-        o_new[part, :] = (acc_old[part, :] * shrink + acc) / total
+        first, second = pl.ds(g * rows, rows), pl.ds((g + 1) * rows, rows)
+        o_new[first, :] = base[first, :] + acc[:rows, :HD]
+        o_new[second, :] = base[second, :] + acc[rows:, HD:]
     mine = mine_mask[...] > 0
     for s in range(steps):
         for g in range(KVH):
@@ -269,6 +283,10 @@
                 fresh = o_new[pl.ds(g * rows + s * SHARE + e, 1), :]
                 tile = part_out[s, :, lanes].astype(jnp.float32)
                 out[s, :, lanes] = jnp.where(mine, fresh, tile).astype(jnp.bfloat16)
+        copies.append(pltpu.make_async_copy(out.at[s], out_hbm.at[s], sems.at[s]))
+        copies[-1].start()
+    for copy in copies:
+        copy.wait()
 
 
 def per_device(
@@ -375,15 +393,35 @@
     pieces_k = spread(own_k, twin_k, got_k)
     pieces_v = spread(own_v, twin_v, got_v)
 
-    landed = jax.ShapeDtypeStruct((1, most_pages * page_rows, width), bf16)
-    return kernel(
-        functools.partial(land_kernel, masks),
-        out_shape=(jax.ShapeDtypeStruct(queries.shape, bf16), landed, landed),
-        in_specs=[VMEM] * (8 + 2 * len(masks)),
+    span = most_pages * page_rows
+    small = pltpu.CompilerParams(vmem_limit_bytes=8 * 2**20)
+    landed_k, weights, base = kernel(
+        functools.partial(land_keys_kernel, masks),
+        out_shape=(
+            jax.ShapeDtypeStruct((span, width), bf16),
+            jax.ShapeDtypeStruct((block, span), bf16),
+            stats,
+        ),
+        in_specs=[VMEM] * (6 + len(masks)),
         out_specs=(VMEM,) * 3,
-        scratch_shapes=[pltpu.VMEM((block, HD), f32)],
-        compiler_params=pltpu.CompilerParams(vmem_limit_bytes=8 * 2**20),
-    )(part_out, q_mine, acc, top, total, land_mask, bias, mine_mask, *pieces_k, *pieces_v)
+        compiler_params=small,
+    )(q_mine, acc, top, total, land_mask, bias, *pieces_k)
+    attended, landed_v = kernel(
+        functools.partial(land_values_kernel, masks),
+        out_shape=(
+            jax.ShapeDtypeStruct(queries.shape, bf16), jax.ShapeDtypeStruct((span, width), bf16)
+        ),
+        in_specs=[VMEM] * (5 + len(masks)),
+        out_specs=(HBM, HBM),
+        scratch_shapes=[
+            pltpu.VMEM(queries.shape, bf16),
+            pltpu.VMEM((span, width), bf16),
+            pltpu.VMEM((block, HD), f32),
+            pltpu.SemaphoreType.DMA((steps + 1,)),
+        ],
+        compiler_params=small,
+    )(part_out, weights, base, land_mask, mine_mask, *pieces_v)
+    return attended, landed_k[None], landed_v[None]
 
 
 def solution(mesh):

time: 30.1 us -> 29.7 us (0.987)
  waiting for transfers between devices: 9.46 us -> 8.59 us
  Pallas kernels: 7.89 us -> 8.31 us
    ppermute x12, waiting for transfers between devices: 9.46 us -> 8.59 us  [swap(): return lax.ppermute(x, 'seq', [(i, i ^ mask) for i in range(chain)])]
    pallas_call x5 -> x6, Pallas kernels: 7.89 us -> 8.31 us  [call(): return pl.pallas_call(body, **settings)(*args)]
  transfers between devices with their start and end apart: 12 -> 12, of which waited for: 6 -> 6; matrix products, arithmetic and copies ran while one was open for 0% -> 0% of each run, Pallas kernels for 21% -> 24%
where the time goes in v1:
time: 29.7 us; the launch traced here: 29.5 us
  starting transfers between devices  11.9 us (40%)
  waiting for transfers between devices  8.59 us (29%)
  Pallas kernels  8.31 us (28%)
  between operations  0.69 us (2%)
    ppermute x12, starting transfers between devices, swap(): return lax.ppermute(x, 'seq', [(i, i ^ mask) for i in range(chain)])  11.9 us
    ppermute x12, waiting for transfers between devices, swap(): return lax.ppermute(x, 'seq', [(i, i ^ mask) for i in range(chain)])  8.59 us
    pallas_call x6, Pallas kernels, call(): return pl.pallas_call(body, **settings)(*args)  8.31 us
  transfers between devices with their start and end apart: 12, of which 6 were waited for; matrix products, arithmetic and copies ran while one was open for 0% of the time, Pallas kernels for 24%

profile of v1, /device:TPU:0, one launch (start us, length us, event | category | flops | bytes accessed | tf_op | source)
XLA Modules:
  0.0 29.5 jit_solution(1179146739659984313)
XLA Ops:
  0.6 4.1 %collective-permute-start = (bf16[4,16,1024]{2,1,0:T(8,128)(2,1)}, bf16[4,16,1024]{2,1,0:T(8,128)(2,1)S(1)}, u32[]{:S(2)}, u32[]{:S(2)}) collective-permute-start(bf16[4,16,1024]{2,1,0:T(8,128)(2,1)} %bitcast.5), channel_id=1, source_target_pairs={{0,8},{1,9},{2,10},{3,11},{4,12},{5,13},{6,14},{7,15},{8,0},{9,1},... | collective-permute-start | bytes 393224 | tf_op jit(solution)/shard_map/ppermute | solution.py:308
  4.8 2.7 %shard_map.130 = (f32[1024,128]{1,0:T(8,128)S(1)}, f32[2,128,128]{2,1,0:T(8,128)S(1)}, bf16[64,16,1024]{2,1,0:T(8,128)(2,1)S(1)}, bf16[64,16,1024]{2,1,0:T(8,128...) custom-call(s32[1]{0:T(128)} %bitcast.1.place, ...), custom_call_target="tpu_custom_call" | custom-call | tf_op jit(solution)/shard_map/pallas_call | solution.py:312
  7.5 0.1 collective-permute-start.7
  7.6 0.1 collective-permute-start.1
  7.7 3.1 %shard_map.131 = (bf16[4,4,8192]{2,1,0:T(4,128)(2,1)S(1)}, bf16[256,256]{1,0:T(8,128)(2,1)S(1)}, f32[256,128]{1,0:T(8,128)S(1)}, f32[256,128]{1,0:T(8,128)S(1)}, f32[256,128]{1,0:T(8,128)S(1)}) custom-call(s32[1]{0:T(128)} %bitcast.1.place, s32[16]{0:T(128)} %turn_lengths_hbm.1, s32[16]{0:T(128)} %turn_slot_hbm.1, s32[4,16]{1,0:T(4,128)} %table_hbm.1, ...), custom_call_target="tpu_custom_call" | custom-call | flops 134217728 | bytes 4194304 | tf_op jit(solution)/shard_map/pallas_call | solution.py:312
  10.7 4.0 %collective-permute-done.got = bf16[4,16,1024]{2,1,0:T(8,128)(2,1)S(1)} collective-permute-done((bf16[4,16,1024]{2,1,0:T(8,128)(2,1)}, bf16[4,16,1024]{2,1,0:T(8,128)(2,1)S(1)}, u32[]{:S(2)}, u32[]{:S(2)}) %collective-permute-start) | collective-permute-done | bytes 131104 | tf_op jit(solution)/shard_map/ppermute | solution.py:308
  14.8 0.0 collective-permute-start.2
  14.8 0.5 %collective-permute-start.6 = (bf16[4,16,1024]{2,1,0:T(8,128)(2,1)S(1)}, bf16[4,16,1024]{2,1,0:T(8,128)(2,1)S(1)}, u32[]{:S(2)}, u32[]{:S(2)}) collective-permute-start(bf16[4,16,1024]{2,1,0:T(8,128)(2,1)S(1)} %bitcast.9), channel_id=1, source_target_pairs={{0,1},{1,0},{2,3},{3,2},{4,5},{5,4},{6,7},{7,6},{8,9},{9,8},{10,11... | collective-permute-start | bytes 393224 | tf_op jit(solution)/shard_map/ppermute | solution.py:308
  15.3 1.6 %collective-permute-done.7.got = bf16[4,16,1024]{2,1,0:T(8,128)(2,1)S(1)} collective-permute-done((bf16[4,16,1024]{2,1,0:T(8,128)(2,1)S(1)}, bf16[4,16,1024]{2,1,0:T(8,128)(2,1)S(1)}, u32[]{:S(2)}, u32[]{:S(2)}) %collective-permute-start.7) | collective-permute-done | bytes 131104 | tf_op jit(solution)/shard_map/ppermute | solution.py:308
  16.9 0.0 collective-permute-start.8
  16.9 0.3 shard_map.132
  17.2 1.6 %collective-permute-start.3 = (bf16[2,16,1024]{2,1,0:T(8,128)(2,1)S(1)}, bf16[2,16,1024]{2,1,0:T(8,128)(2,1)S(1)}, u32[]{:S(2)}, u32[]{:S(2)}) collective-permute-start(bf16[2,16,1024]{2,1,0:T(8,128)(2,1)S(1)} %get-tuple-element.49), channel_id=1, source_target_pairs={{0,2},{1,3},{2,0},{3,1},{4,6},{5,7},{6,4},{7,5},{8,10},{9,11},{10,... | collective-permute-start | bytes 196616 | tf_op jit(solution)/shard_map/ppermute | solution.py:308
  18.8 0.7 %collective-permute-start.4 = (bf16[2,16,1024]{2,1,0:T(8,128)(2,1)S(1)}, bf16[2,16,1024]{2,1,0:T(8,128)(2,1)S(1)}, u32[]{:S(2)}, u32[]{:S(2)}) collective-permute-start(bf16[2,16,1024]{2,1,0:T(8,128)(2,1)S(1)} %get-tuple-element.50), channel_id=1, source_target_pairs={{0,4},{1,5},{2,6},{3,7},{4,0},{5,1},{6,2},{7,3},{8,12},{9,13},{10,... | collective-permute-start | bytes 196616 | tf_op jit(solution)/shard_map/ppermute | solution.py:308
  19.5 1.2 %collective-permute-start.5 = (bf16[2,16,1024]{2,1,0:T(8,128)(2,1)S(1)}, bf16[2,16,1024]{2,1,0:T(8,128)(2,1)S(1)}, u32[]{:S(2)}, u32[]{:S(2)}) collective-permute-start(bf16[2,16,1024]{2,1,0:T(8,128)(2,1)S(1)} %get-tuple-element.51), channel_id=1, source_target_pairs={{0,6},{1,7},{2,4},{3,5},{4,2},{5,3},{6,0},{7,1},{8,14},{9,15},{10,... | collective-permute-start | bytes 196616 | tf_op jit(solution)/shard_map/ppermute | solution.py:308
  20.7 0.3 shard_map.134
  21.0 0.8 %collective-permute-start.10 = (bf16[2,16,1024]{2,1,0:T(8,128)(2,1)S(1)}, bf16[2,16,1024]{2,1,0:T(8,128)(2,1)S(1)}, u32[]{:S(2)}, u32[]{:S(2)}) collective-permute-start(bf16[2,16,1024]{2,1,0:T(8,128)(2,1)S(1)} %get-tuple-element.58), channel_id=1, source_target_pairs={{0,4},{1,5},{2,6},{3,7},{4,0},{5,1},{6,2},{7,3},{8,12},{9,13},{10,... | collective-permute-start | bytes 196616 | tf_op jit(solution)/shard_map/ppermute | solution.py:308
  21.8 2.3 %collective-permute-start.11 = (bf16[2,16,1024]{2,1,0:T(8,128)(2,1)S(1)}, bf16[2,16,1024]{2,1,0:T(8,128)(2,1)S(1)}, u32[]{:S(2)}, u32[]{:S(2)}) collective-permute-start(bf16[2,16,1024]{2,1,0:T(8,128)(2,1)S(1)} %get-tuple-element.59), channel_id=1, source_target_pairs={{0,6},{1,7},{2,4},{3,5},{4,2},{5,3},{6,0},{7,1},{8,14},{9,15},{10,... | collective-permute-start | bytes 196616 | tf_op jit(solution)/shard_map/ppermute | solution.py:308
  24.1 0.5 %collective-permute-start.9 = (bf16[2,16,1024]{2,1,0:T(8,128)(2,1)S(1)}, bf16[2,16,1024]{2,1,0:T(8,128)(2,1)S(1)}, u32[]{:S(2)}, u32[]{:S(2)}) collective-permute-start(bf16[2,16,1024]{2,1,0:T(8,128)(2,1)S(1)} %get-tuple-element.57), channel_id=1, source_target_pairs={{0,2},{1,3},{2,0},{3,1},{4,6},{5,7},{6,4},{7,5},{8,10},{9,11},{10,... | collective-permute-start | bytes 196616 | tf_op jit(solution)/shard_map/ppermute | solution.py:308
  24.6 0.4 %collective-permute-done.5.refs_3_ = bf16[2,16,1024]{2,1,0:T(8,128)(2,1)S(1)} collective-permute-done((bf16[2,16,1024]{2,1,0:T(8,128)(2,1)S(1)}, bf16[2,16,1024]{2,1,0:T(8,128)(2,1)S(1)}, u32[]{:S(2)}, u32[]{:S(2)}) %collective-permute-start.5) | collective-permute-done | bytes 65568 | tf_op jit(solution)/shard_map/ppermute | solution.py:308
  25.0 0.9 %shard_map.133 = (bf16[80,1024]{1,0:T(8,128)(2,1)}, bf16[256,80]{1,0:T(8,128)(2,1)S(1)}, f32[256,128]{1,0:T(8,128)S(1)}) custom-call(bf16[256,256]{1,0:T(8,128)(2,1)S(1)} %get-tuple-element.40.q, f32[256,128]{1,0:T(8,128)S(1)} %get-tuple-element.41.acc_old, f32[256,128]{1,0:T(8,128)S(1)} %get-tuple-element.42.max_old, ...), custom_call_target="tpu_custom_call" | custom-call | tf_op jit(solution)/shard_map/pallas_call | solution.py:312
  25.9 0.7 %collective-permute-done.10.refs_2_ = bf16[2,16,1024]{2,1,0:T(8,128)(2,1)S(1)} collective-permute-done((bf16[2,16,1024]{2,1,0:T(8,128)(2,1)S(1)}, bf16[2,16,1024]{2,1,0:T(8,128)(2,1)S(1)}, u32[]{:S(2)}, u32[]{:S(2)}) %collective-permute-start.10) | collective-permute-done | bytes 65568 | tf_op jit(solution)/shard_map/ppermute | solution.py:308
  26.5 1.0 %collective-permute-done.11.refs_3_ = bf16[2,16,1024]{2,1,0:T(8,128)(2,1)S(1)} collective-permute-done((bf16[2,16,1024]{2,1,0:T(8,128)(2,1)S(1)}, bf16[2,16,1024]{2,1,0:T(8,128)(2,1)S(1)}, u32[]{:S(2)}, u32[]{:S(2)}) %collective-permute-start.11) | collective-permute-done | bytes 65568 | tf_op jit(solution)/shard_map/ppermute | solution.py:308
  27.6 0.8 %collective-permute-done.9.refs_1_ = bf16[2,16,1024]{2,1,0:T(8,128)(2,1)S(1)} collective-permute-done((bf16[2,16,1024]{2,1,0:T(8,128)(2,1)S(1)}, bf16[2,16,1024]{2,1,0:T(8,128)(2,1)S(1)}, u32[]{:S(2)}, u32[]{:S(2)}) %collective-permute-start.9) | collective-permute-done | bytes 65568 | tf_op jit(solution)/shard_map/ppermute | solution.py:308
  28.4 1.1 %shard_map.135 = (bf16[4,4,8192]{2,1,0:T(4,128)(2,1)}, bf16[80,1024]{1,0:T(8,128)(2,1)}) custom-call(bf16[4,4,8192]{2,1,0:T(4,128)(2,1)S(1)} %get-tuple-element.39.part_out, bf16[256,80]{1,0:T(8,128)(2,1)S(1)} %get-tuple-element.52.weights, f32[256,128]{1,0:T(8,128)S(1)} %get-tuple-element.53.base, bf16[5,8,16,128]{3,2,1,0:T(8,128)(2,1)S(1)} %get-tuple-element.44.land_mask, ...), custom_call_target="tpu_custom_call" | custom-call | tf_op jit(solution)/shard_map/pallas_call | solution.py:312
  (10 shorter events, 0.0 us)
Async XLA Ops:
  0.6 14.1 %collective-permute-start = (bf16[4,16,1024]{2,1,0:T(8,128)(2,1)}, bf16[4,16,1024]{2,1,0:T(8,128)(2,1)S(1)}, u32[]{:S(2)}, u32[]{:S(2)}) collective-permute-start(bf16[4,16,1024]{2,1,0:T(8,128)(2,1)} %bitcast.5), channel_id=1, source_target_pairs={{0,8},{1,9},{2,10},{3,11},{4,12},{5,13},{6,14},{7,15},{8,0},{9,1},... | collective-permute-start | bytes 393224 | tf_op jit(solution)/shard_map/ppermute | solution.py:308
  4.8 2.7 %copy-start.1 = (bf16[4,1,16,1024]{3,2,1,0:T(8,128)(2,1)S(1)}, bf16[4,1,16,1024]{3,2,1,0:T(8,128)(2,1)}, u32[]{:S(2)}) copy-start(bf16[4,1,16,1024]{3,2,1,0:T(8,128)(2,1)} %param.19) | copy-start | bytes 393220
  4.8 2.8 %copy-start = (bf16[4,1,16,1024]{3,2,1,0:T(8,128)(2,1)S(1)}, bf16[4,1,16,1024]{3,2,1,0:T(8,128)(2,1)}, u32[]{:S(2)}) copy-start(bf16[4,1,16,1024]{3,2,1,0:T(8,128)(2,1)} %param.18) | copy-start | bytes 393220
  7.5 9.4 %collective-permute-start.7 = (bf16[4,16,1024]{2,1,0:T(8,128)(2,1)S(1)}, bf16[4,16,1024]{2,1,0:T(8,128)(2,1)S(1)}, u32[]{:S(2)}, u32[]{:S(2)}) collective-permute-start(bf16[4,16,1024]{2,1,0:T(8,128)(2,1)S(1)} %bitcast.8), channel_id=1, source_target_pairs={{0,8},{1,9},{2,10},{3,11},{4,12},{5,13},{6,14},{7,15},{8,0},{9,1},... | collective-permute-start | bytes 393224 | tf_op jit(solution)/shard_map/ppermute | solution.py:308
  7.6 9.3 %collective-permute-start.1 = (bf16[4,16,1024]{2,1,0:T(8,128)(2,1)S(1)}, bf16[4,16,1024]{2,1,0:T(8,128)(2,1)S(1)}, u32[]{:S(2)}, u32[]{:S(2)}) collective-permute-start(bf16[4,16,1024]{2,1,0:T(8,128)(2,1)S(1)} %bitcast.6), channel_id=1, source_target_pairs={{0,1},{1,0},{2,3},{3,2},{4,5},{5,4},{6,7},{7,6},{8,9},{9,8},{10,11... | collective-permute-start | bytes 393224 | tf_op jit(solution)/shard_map/ppermute | solution.py:308
  14.8 2.1 %collective-permute-start.2 = (bf16[4,16,1024]{2,1,0:T(8,128)(2,1)S(1)}, bf16[4,16,1024]{2,1,0:T(8,128)(2,1)S(1)}, u32[]{:S(2)}, u32[]{:S(2)}) collective-permute-start(bf16[4,16,1024]{2,1,0:T(8,128)(2,1)S(1)} %collective-permute-done.got), channel_id=1, source_target_pairs={{0,1},{1,0},{2,3},{3,2},{4,5},{5,4},{6,7},{7,6},{8,9},{9,8},{10,11... | collective-permute-start | bytes 393224 | tf_op jit(solution)/shard_map/ppermute | solution.py:308
  14.8 6.0 %collective-permute-start.6 = (bf16[4,16,1024]{2,1,0:T(8,128)(2,1)S(1)}, bf16[4,16,1024]{2,1,0:T(8,128)(2,1)S(1)}, u32[]{:S(2)}, u32[]{:S(2)}) collective-permute-start(bf16[4,16,1024]{2,1,0:T(8,128)(2,1)S(1)} %bitcast.9), channel_id=1, source_target_pairs={{0,1},{1,0},{2,3},{3,2},{4,5},{5,4},{6,7},{7,6},{8,9},{9,8},{10,11... | collective-permute-start | bytes 393224 | tf_op jit(solution)/shard_map/ppermute | solution.py:308
  16.9 3.8 %collective-permute-start.8 = (bf16[4,16,1024]{2,1,0:T(8,128)(2,1)S(1)}, bf16[4,16,1024]{2,1,0:T(8,128)(2,1)S(1)}, u32[]{:S(2)}, u32[]{:S(2)}) collective-permute-start(bf16[4,16,1024]{2,1,0:T(8,128)(2,1)S(1)} %collective-permute-done.7.got), channel_id=1, source_target_pairs={{0,1},{1,0},{2,3},{3,2},{4,5},{5,4},{6,7},{7,6},{8,9},{9,8},{10,11... | collective-permute-start | bytes 393224 | tf_op jit(solution)/shard_map/ppermute | solution.py:308
  17.2 6.9 %collective-permute-start.3 = (bf16[2,16,1024]{2,1,0:T(8,128)(2,1)S(1)}, bf16[2,16,1024]{2,1,0:T(8,128)(2,1)S(1)}, u32[]{:S(2)}, u32[]{:S(2)}) collective-permute-start(bf16[2,16,1024]{2,1,0:T(8,128)(2,1)S(1)} %get-tuple-element.49), channel_id=1, source_target_pairs={{0,2},{1,3},{2,0},{3,1},{4,6},{5,7},{6,4},{7,5},{8,10},{9,11},{10,... | collective-permute-start | bytes 196616 | tf_op jit(solution)/shard_map/ppermute | solution.py:308
  18.8 5.8 %collective-permute-start.4 = (bf16[2,16,1024]{2,1,0:T(8,128)(2,1)S(1)}, bf16[2,16,1024]{2,1,0:T(8,128)(2,1)S(1)}, u32[]{:S(2)}, u32[]{:S(2)}) collective-permute-start(bf16[2,16,1024]{2,1,0:T(8,128)(2,1)S(1)} %get-tuple-element.50), channel_id=1, source_target_pairs={{0,4},{1,5},{2,6},{3,7},{4,0},{5,1},{6,2},{7,3},{8,12},{9,13},{10,... | collective-permute-start | bytes 196616 | tf_op jit(solution)/shard_map/ppermute | solution.py:308
  19.5 5.5 %collective-permute-start.5 = (bf16[2,16,1024]{2,1,0:T(8,128)(2,1)S(1)}, bf16[2,16,1024]{2,1,0:T(8,128)(2,1)S(1)}, u32[]{:S(2)}, u32[]{:S(2)}) collective-permute-start(bf16[2,16,1024]{2,1,0:T(8,128)(2,1)S(1)} %get-tuple-element.51), channel_id=1, source_target_pairs={{0,6},{1,7},{2,4},{3,5},{4,2},{5,3},{6,0},{7,1},{8,14},{9,15},{10,... | collective-permute-start | bytes 196616 | tf_op jit(solution)/shard_map/ppermute | solution.py:308
  21.0 5.5 %collective-permute-start.10 = (bf16[2,16,1024]{2,1,0:T(8,128)(2,1)S(1)}, bf16[2,16,1024]{2,1,0:T(8,128)(2,1)S(1)}, u32[]{:S(2)}, u32[]{:S(2)}) collective-permute-start(bf16[2,16,1024]{2,1,0:T(8,128)(2,1)S(1)} %get-tuple-element.58), channel_id=1, source_target_pairs={{0,4},{1,5},{2,6},{3,7},{4,0},{5,1},{6,2},{7,3},{8,12},{9,13},{10,... | collective-permute-start | bytes 196616 | tf_op jit(solution)/shard_map/ppermute | solution.py:308
  21.8 5.8 %collective-permute-start.11 = (bf16[2,16,1024]{2,1,0:T(8,128)(2,1)S(1)}, bf16[2,16,1024]{2,1,0:T(8,128)(2,1)S(1)}, u32[]{:S(2)}, u32[]{:S(2)}) collective-permute-start(bf16[2,16,1024]{2,1,0:T(8,128)(2,1)S(1)} %get-tuple-element.59), channel_id=1, source_target_pairs={{0,6},{1,7},{2,4},{3,5},{4,2},{5,3},{6,0},{7,1},{8,14},{9,15},{10,... | collective-permute-start | bytes 196616 | tf_op jit(solution)/shard_map/ppermute | solution.py:308
  24.1 4.3 %collective-permute-start.9 = (bf16[2,16,1024]{2,1,0:T(8,128)(2,1)S(1)}, bf16[2,16,1024]{2,1,0:T(8,128)(2,1)S(1)}, u32[]{:S(2)}, u32[]{:S(2)}) collective-permute-start(bf16[2,16,1024]{2,1,0:T(8,128)(2,1)S(1)} %get-tuple-element.57), channel_id=1, source_target_pairs={{0,2},{1,3},{2,0},{3,1},{4,6},{5,7},{6,4},{7,5},{8,10},{9,11},{10,... | collective-permute-start | bytes 196616 | tf_op jit(solution)/shard_map/ppermute | solution.py:308

commit v2 on v1

--- a/solution.py
+++ b/solution.py
@@ -48,10 +48,11 @@
 ):
     ints_hbm, refs = refs[:ints], refs[ints:]
     q_hbm, new_k_hbm, new_v_hbm, pool_k, pool_v = refs[:5]
-    q_all, new_all, k_buf, v_buf, pick_mask, land_mask, bias, mine_mask = refs[5:13]
-    q, new_k, new_v = refs[13:16]
-    turn_lengths, turn_slot = refs[16 : 16 + ints]
-    sems = refs[16 + ints]
+    q_all, new_all, s_new, k_buf, v_buf = refs[5:10]
+    pick_k, pick_v, land_mask, bias, mine_mask = refs[10:15]
+    q, new_k, new_v = refs[15:18]
+    turn_lengths, turn_slot = refs[18 : 18 + ints]
+    starts, counts, tokens_of, slot_of, sems = refs[18 + ints :]
     steps, slots, _ = q.shape
     page_rows = k_buf.shape[1]
     rows = steps * SHARE
@@ -61,26 +62,43 @@
         (q_hbm, q), (new_k_hbm, new_k), (new_v_hbm, new_v), (pool_k, k_buf), (pool_v, v_buf),
     )
     copies = [pltpu.make_async_copy(*pair, sems.at[i]) for i, pair in enumerate(pairs)]
-    for copy in copies:
+    for copy in copies[:5]:
         copy.start()
     for copy in copies[:2]:
         copy.wait()
+    for copy in copies[5:]:
+        copy.start()
 
     me = place[0]
+
+    def note(t, first):
+        tokens = turn_lengths[t]
+        owner = turn_slot[t] // slots
+        counted = (tokens + page_rows - 1) // page_rows
+        starts[owner] = first
+        counts[owner] = counted
+        tokens_of[owner] = tokens
+        slot_of[owner] = turn_slot[t] % slots
+        return first + counted
+
+    lax.fori_loop(0, turn_lengths.shape[0], note, jnp.int32(0), unroll=4)
     row = lax.broadcasted_iota(jnp.int32, (page_rows, HD), 0)
     for i, mask in enumerate(masks):
-        start, count, _, _ = turn_of(turn_lengths, turn_slot, page_rows, slots, me ^ mask)
         for slot in range(2):
-            residue = me ^ slot
-            page = start + ((residue - start) & (half - 1))
-            for side in range(2):
-                for lap in range(laps):
-                    wanted = lap * chain + (residue ^ (side * half))
-                    hit = (page == wanted) & (page < start + count)
-                    pick_mask[((i * 2 + slot) * 2 + side) * laps + lap] = jnp.full(
-                        (page_rows, HD), hit.astype(jnp.float32)
-                    ).astype(jnp.bfloat16)
-    start, count, length, my_slot = turn_of(turn_lengths, turn_slot, page_rows, slots, me)
+            start, count = starts[me ^ mask ^ slot], counts[me ^ mask ^ slot]
+            for pick, residues in ((pick_k, (0,)), (pick_v, (0, 1)[: 2 - 2 * slot])):
+                for twin in residues:
+                    residue = me ^ twin
+                    page = start + ((residue - start) & (half - 1))
+                    for side in range(2):
+                        for lap in range(laps):
+                            wanted = lap * chain + (residue ^ (side * half))
+                            hit = (page == wanted) & (page < start + count)
+                            line = i * 2 + (slot if pick is pick_k else twin)
+                            pick[(line * 2 + side) * laps + lap] = jnp.full(
+                                (page_rows, HD), hit.astype(jnp.float32)
+                            ).astype(jnp.bfloat16)
+    start, length, my_slot = starts[me], tokens_of[me], slot_of[me]
     for j in range(land_mask.shape[0]):
         kept = (row + j * page_rows < length).astype(jnp.float32)
         for i, mask in enumerate(masks):
@@ -106,28 +124,6 @@
             for e in range(SHARE):
                 tile = q[s, :, pl.ds((g * SHARE + e) * HD, HD)].astype(jnp.float32)
                 q_all[pl.ds(g * rows + s * SHARE + e, slots, stride=KVH * rows), :] = tile
-    for copy in copies[5:]:
-        copy.wait()
-
-
-def resident_kernel(
-    place, turn_lengths_hbm, turn_slot_hbm, table_hbm, lengths_hbm, q_all, new_all, k_buf, v_buf,
-    out, q_mine, acc_mine, max_mine, sum_mine,
-    turn_lengths, turn_slot, table, lengths, s_new, p_new, acc_all, max_all, sum_all, sems,
-):
-    steps, slots, _ = out.shape
-    page_rows = k_buf.shape[1]
-    pages = table.shape[1]
-    span = pages * page_rows
-    rows = steps * SHARE
-    pairs = (
-        (turn_lengths_hbm, turn_lengths), (turn_slot_hbm, turn_slot),
-        (table_hbm, table), (lengths_hbm, lengths),
-    )
-    copies = [pltpu.make_async_copy(*pair, sems.at[i]) for i, pair in enumerate(pairs)]
-    for copy in copies:
-        copy.start()
-
     fresh = (steps * KVH * slots, HD)
     block = KVH * rows
     column = lax.broadcasted_iota(jnp.int32, (block, fresh[0]), 1)
@@ -144,6 +140,29 @@
             preferred_element_type=jnp.float32,
         )
         s_new[part, :] = jnp.where(causal & (column_slot == r), score * LOG2_SCALE, -jnp.inf)
+    for copy in copies[5:]:
+        copy.wait()
+
+
+def resident_kernel(
+    place, turn_lengths_hbm, turn_slot_hbm, table_hbm, lengths_hbm,
+    q_all, new_all, s_new, k_buf, v_buf,
+    out, q_mine, acc_mine, max_mine, sum_mine,
+    turn_lengths, turn_slot, table, lengths, p_new, acc_all, max_all, sum_all, sems,
+):
+    steps, slots, _ = out.shape
+    page_rows = k_buf.shape[1]
+    pages = table.shape[1]
+    span = pages * page_rows
+    rows = steps * SHARE
+    block = KVH * rows
+    pairs = (
+        (turn_lengths_hbm, turn_lengths), (turn_slot_hbm, turn_slot),
+        (table_hbm, table), (lengths_hbm, lengths),
+    )
+    copies = [pltpu.make_async_copy(*pair, sems.at[i]) for i, pair in enumerate(pairs)]
+    for copy in copies:
+        copy.start()
 
     token = lax.broadcasted_iota(jnp.int32, (2 * rows, span), 1)
     none = jnp.zeros((rows, HD), jnp.bfloat16)
@@ -207,12 +226,15 @@
                 out[s, :, pl.ds((g * SHARE + e) * HD, HD)] = tile.astype(jnp.bfloat16)
 
 
-def pick_kernel(laps, pick_mask, own, twin, got, got_twin, *outs):
-    width = own.shape[2]
+def pick_kernel(laps, masks, pick_mask, *refs):
+    sources, outs = refs[: -len(masks)], refs[-len(masks) :]
+    pairs = [sources[i : i + 2] for i in range(0, len(sources), 2)]
+    width = sources[0].shape[2]
     for i, out in enumerate(outs):
-        for slot, sides in enumerate(((own, got), (twin, got_twin))):
+        for line in range(2):
+            sides = pairs[line % len(pairs)]
             hits = [
-                pick_mask[((i * 2 + slot) * 2 + side) * laps + lap] > 0
+                pick_mask[((i * 2 + line) * 2 + side) * laps + lap] > 0
                 for side in range(2)
                 for lap in range(laps)
             ]
@@ -222,25 +244,32 @@
                 best = jnp.zeros_like(pages[0])
                 for hit, page in zip(hits, pages):
                     best = jnp.where(hit, page, best)
-                out[slot, :, lanes] = best
+                out[line, :, lanes] = best
+
+
+def join_kernel(*refs):
+    for i, piece in enumerate(refs[:-1]):
+        refs[-1][i] = piece[1]
 
 
 def place_pages(land_mask, pieces, landed):
     pages, _, page_rows, _ = land_mask.shape
     for j in range(pages):
-        hits = [land_mask[j, i] > 0 for i in range(2 * len(pieces))]
+        hits = [land_mask[j, i] > 0 for i in range(len(pieces))]
         for lane in range(0, landed.shape[1], HD):
             lanes = pl.ds(lane, HD)
             found = jnp.zeros((page_rows, HD), jnp.bfloat16)
             for i, hit in enumerate(hits):
-                found = jnp.where(hit, pieces[i // 2][i % 2, :, lanes], found)
+                piece, line = pieces[i]
+                found = jnp.where(hit, piece[line, :, lanes], found)
             landed[pl.ds(j * page_rows, page_rows), lanes] = found
 
 
 def land_keys_kernel(masks, q, acc_old, max_old, sum_old, land_mask, bias, *refs):
-    pieces = refs[: len(masks)]
-    landed, weights, base = refs[len(masks) :]
-    place_pages(land_mask, pieces, landed)
+    pieces, other = refs[: len(masks)], refs[len(masks)]
+    landed, weights, base = refs[len(masks) + 1 :]
+    lines = [line for i, piece in enumerate(pieces) for line in ((piece, 0), (other, i))]
+    place_pages(land_mask, lines, landed)
     rows = q.shape[0] // KVH
     span = landed.shape[0]
     for g in range(0, KVH, 2):
@@ -264,7 +293,7 @@
     out_hbm, landed_hbm, out, landed, o_new, sems = refs[len(masks) :]
     steps = out.shape[0]
     rows = steps * SHARE
-    place_pages(land_mask, pieces, landed)
+    place_pages(land_mask, [(piece, line) for piece in pieces for line in range(2)], landed)
     copies = [pltpu.make_async_copy(landed, landed_hbm, sems.at[steps])]
     copies[0].start()
     for g in range(0, KVH, 2):
@@ -327,31 +356,35 @@
         return tuple(pltpu.with_memory_space_constraint(x, pltpu.HBM) for x in arrays)
 
     got_k = swap(own_k, half)
-    twin_k, twin_v = swap(own_k, 1), swap(own_v, 1)
+    twin_v = swap(own_v, 1)
     large = in_hbm(queries, new_keys, new_values, pool_keys, pool_values)
     ints = in_hbm(turn_lengths, turn_slot)
     more_ints = in_hbm(page_table, cached_len)
-    q_all, new_all, k_buf, v_buf, pick_mask, land_mask, bias, mine_mask = kernel(
+    q_all, new_all, s_new, k_buf, v_buf, *tables = kernel(
         functools.partial(prepare_kernel, chain, masks, laps, len(ints)),
         out_shape=(
             jax.ShapeDtypeStruct((slots * block, HD), f32),
             jax.ShapeDtypeStruct((2, *fresh), f32),
+            jax.ShapeDtypeStruct((slots * block, fresh[0]), f32),
             jax.ShapeDtypeStruct(pool_keys.shape, bf16),
             jax.ShapeDtypeStruct(pool_values.shape, bf16),
+            jax.ShapeDtypeStruct((len(masks) * 4 * laps, page_rows, HD), bf16),
             jax.ShapeDtypeStruct((len(masks) * 4 * laps, page_rows, HD), bf16),
             jax.ShapeDtypeStruct((most_pages, 2 * len(masks), page_rows, HD), bf16),
             jax.ShapeDtypeStruct((2 * rows, HD), f32),
             jax.ShapeDtypeStruct((slots, HD), f32),
         ),
         in_specs=[SMEM] + [HBM] * 7,
-        out_specs=(VMEM,) * 8,
+        out_specs=(VMEM,) * 10,
         scratch_shapes=[
             *(pltpu.VMEM(x.shape, bf16) for x in large[:3]),
             *(pltpu.SMEM(x.shape, jnp.int32) for x in ints),
+            *(pltpu.SMEM((chain,), jnp.int32) for _ in range(4)),
             pltpu.SemaphoreType.DMA((7,)),
         ],
         compiler_params=pltpu.CompilerParams(vmem_limit_bytes=16 * 2**20),
     )(place, *ints, *large)
+    mask_k, mask_v, land_mask, bias, mine_mask = tables
     own_v, q_all = lax.optimization_barrier((own_v, q_all))
     got_v = swap(own_v, half)
     part_out, q_mine, acc, top, total = kernel(
@@ -361,11 +394,10 @@
             jax.ShapeDtypeStruct((block, 2 * HD), bf16),
             stats, stats, stats,
         ),
-        in_specs=[SMEM] + [HBM] * 4 + [VMEM] * 4,
+        in_specs=[SMEM] + [HBM] * 4 + [VMEM] * 5,
         out_specs=(VMEM,) * 5,
         scratch_shapes=[
             *(pltpu.SMEM(x.shape, jnp.int32) for x in ints + more_ints),
-            all_rows,
             pltpu.VMEM((slots * block, HD), bf16),
             all_rows, all_rows, all_rows,
             pltpu.SemaphoreType.DMA((4,)),
@@ -375,26 +407,34 @@
             flops=4 * slots * block * pages * page_rows * HD,
             bytes_accessed=2 * pool_keys.size * 2, transcendentals=0,
         ),
-    )(place, *ints, *more_ints, q_all, new_all, k_buf, v_buf)
+    )(place, *ints, *more_ints, q_all, new_all, s_new, k_buf, v_buf)
 
     piece = jax.ShapeDtypeStruct((2, page_rows, width), bf16)
-
-    def spread(own, twin, got):
+    small = pltpu.CompilerParams(vmem_limit_bytes=8 * 2**20)
+
+    def spread(*operands):
         picked = kernel(
-            functools.partial(pick_kernel, laps),
+            functools.partial(pick_kernel, laps, masks),
             out_shape=(piece,) * len(masks),
-            in_specs=[VMEM] * 5,
+            in_specs=[VMEM] * len(operands),
             out_specs=(VMEM,) * len(masks),
-            compiler_params=pltpu.CompilerParams(vmem_limit_bytes=8 * 2**20),
-        )(pick_mask, own, twin, got, swap(got, 1))
+            compiler_params=small,
+        )(*operands)
         return [picked[0]] + [swap(x, mask) for x, mask in zip(picked[1:], masks[1:])]
 
     got_k, part_out = lax.optimization_barrier((got_k, part_out))
-    pieces_k = spread(own_k, twin_k, got_k)
-    pieces_v = spread(own_v, twin_v, got_v)
+    pieces_k = spread(mask_k, own_k, got_k)
+    pieces_v = spread(mask_v, own_v, got_v, twin_v, swap(got_v, 1))
+    joined = kernel(
+        join_kernel,
+        out_shape=jax.ShapeDtypeStruct((len(masks), page_rows, width), bf16),
+        in_specs=[VMEM] * len(masks),
+        out_specs=VMEM,
+        compiler_params=small,
+    )(*pieces_k)
+    other_k = swap(joined, 1)
 
     span = most_pages * page_rows
-    small = pltpu.CompilerParams(vmem_limit_bytes=8 * 2**20)
     landed_k, weights, base = kernel(
         functools.partial(land_keys_kernel, masks),
         out_shape=(
@@ -402,10 +442,10 @@
             jax.ShapeDtypeStruct((block, span), bf16),
             stats,
         ),
-        in_specs=[VMEM] * (6 + len(masks)),
+        in_specs=[VMEM] * (7 + len(masks)),
         out_specs=(VMEM,) * 3,
         compiler_params=small,
-    )(q_mine, acc, top, total, land_mask, bias, *pieces_k)
+    )(q_mine, acc, top, total, land_mask, bias, *pieces_k, other_k)
     attended, landed_v = kernel(
         functools.partial(land_values_kernel, masks),
         out_shape=(

time: 29.7 us -> 30.1 us (1.013)
  waiting for transfers between devices: 8.59 us -> 7.05 us
  starting transfers between devices: 11.9 us -> 13.4 us
  Pallas kernels: 8.31 us -> 8.85 us
    ppermute x12 -> x11, waiting for transfers between devices: 8.59 us -> 7.05 us  [swap(): return lax.ppermute(x, 'seq', [(i, i ^ mask) for i in range(chain)])]
    ppermute x12 -> x11, starting transfers between devices: 11.9 us -> 13.4 us  [swap(): return lax.ppermute(x, 'seq', [(i, i ^ mask) for i in range(chain)])]
    pallas_call x6 -> x7, Pallas kernels: 8.31 us -> 8.85 us  [call(): return pl.pallas_call(body, **settings)(*args)]
  transfers between devices with their start and end apart: 12 -> 11, of which waited for: 6 -> 5; matrix products, arithmetic and copies ran while one was open for 0% -> 0% of each run, Pallas kernels for 24% -> 26%
where the time goes in v2:
time: 30.1 us; the launch traced here: 30 us
  starting transfers between devices  13.4 us (45%)
  Pallas kernels  8.85 us (29%)
  waiting for transfers between devices  7.05 us (23%)
  between operations  0.7 us (2%)
    ppermute x11, starting transfers between devices, swap(): return lax.ppermute(x, 'seq', [(i, i ^ mask) for i in range(chain)])  13.4 us
    pallas_call x7, Pallas kernels, call(): return pl.pallas_call(body, **settings)(*args)  8.85 us
    ppermute x11, waiting for transfers between devices, swap(): return lax.ppermute(x, 'seq', [(i, i ^ mask) for i in range(chain)])  7.05 us
  transfers between devices with their start and end apart: 11, of which 5 were waited for; matrix products, arithmetic and copies ran while one was open for 0% of the time, Pallas kernels for 26%

profile of v2, /device:TPU:0, one launch (start us, length us, event | category | flops | bytes accessed | tf_op | source)
XLA Modules:
  0.0 30.0 jit_solution(8459960753077520124)
XLA Ops:
  0.6 4.1 %collective-permute-start = (bf16[4,16,1024]{2,1,0:T(8,128)(2,1)}, bf16[4,16,1024]{2,1,0:T(8,128)(2,1)S(1)}, u32[]{:S(2)}, u32[]{:S(2)}) collective-permute-start(bf16[4,16,1024]{2,1,0:T(8,128)(2,1)} %bitcast.5), channel_id=1, source_target_pairs={{0,8},{1,9},{2,10},{3,11},{4,12},{5,13},{6,14},{7,15},{8,0},{9,1},... | collective-permute-start | bytes 393224 | tf_op jit(solution)/shard_map/ppermute | solution.py:337
  4.8 3.1 %shard_map.130 = (f32[1024,128]{1,0:T(8,128)S(1)}, f32[2,128,128]{2,1,0:T(8,128)S(1)}, f32[1024,128]{1,0:T(8,128)S(1)}, bf16[64,16,1024]{2,1,0:T(8,128)(2,1)S(1)...) custom-call(s32[1]{0:T(128)} %bitcast.1.place, ...), custom_call_target="tpu_custom_call" | custom-call | tf_op jit(solution)/shard_map/pallas_call | solution.py:341
  7.9 0.1 collective-permute-start.5
  8.0 3.2 %shard_map.131 = (bf16[4,4,8192]{2,1,0:T(4,128)(2,1)S(1)}, bf16[256,256]{1,0:T(8,128)(2,1)S(1)}, f32[256,128]{1,0:T(8,128)S(1)}, f32[256,128]{1,0:T(8,128)S(1)}, f32[256,128]{1,0:T(8,128)S(1)}) custom-call(s32[1]{0:T(128)} %bitcast.1.place, s32[16]{0:T(128)} %turn_lengths_hbm.1, s32[16]{0:T(128)} %turn_slot_hbm.1, s32[4,16]{1,0:T(4,128)} %table_hbm.1, ...), custom_call_target="tpu_custom_call" | custom-call | flops 134217728 | bytes 4194304 | tf_op jit(solution)/shard_map/pallas_call | solution.py:341
  11.2 0.3 %collective-permute-done.refs_1_ = bf16[4,16,1024]{2,1,0:T(8,128)(2,1)S(1)} collective-permute-done((bf16[4,16,1024]{2,1,0:T(8,128)(2,1)}, bf16[4,16,1024]{2,1,0:T(8,128)(2,1)S(1)}, u32[]{:S(2)}, u32[]{:S(2)}) %collective-permute-start) | collective-permute-done | bytes 131104 | tf_op jit(solution)/shard_map/ppermute | solution.py:337
  11.6 0.3 shard_map.132
  11.8 1.7 %collective-permute-start.1 = (bf16[2,16,1024]{2,1,0:T(8,128)(2,1)S(1)}, bf16[2,16,1024]{2,1,0:T(8,128)(2,1)S(1)}, u32[]{:S(2)}, u32[]{:S(2)}) collective-permute-start(bf16[2,16,1024]{2,1,0:T(8,128)(2,1)S(1)} %get-tuple-element.52), channel_id=1, source_target_pairs={{0,2},{1,3},{2,0},{3,1},{4,6},{5,7},{6,4},{7,5},{8,10},{9,11},{10,... | collective-permute-start | bytes 196616 | tf_op jit(solution)/shard_map/ppermute | solution.py:337
  13.5 3.4 %collective-permute-start.2 = (bf16[2,16,1024]{2,1,0:T(8,128)(2,1)S(1)}, bf16[2,16,1024]{2,1,0:T(8,128)(2,1)S(1)}, u32[]{:S(2)}, u32[]{:S(2)}) collective-permute-start(bf16[2,16,1024]{2,1,0:T(8,128)(2,1)S(1)} %get-tuple-element.53), channel_id=1, source_target_pairs={{0,4},{1,5},{2,6},{3,7},{4,0},{5,1},{6,2},{7,3},{8,12},{9,13},{10,... | collective-permute-start | bytes 196616 | tf_op jit(solution)/shard_map/ppermute | solution.py:337
  16.9 0.0 collective-permute-start.3
  16.9 0.0 collective-permute-start.6
  16.9 0.0 collective-permute-done.5.refs_1_
  16.9 0.5 %collective-permute-start.7 = (bf16[4,16,1024]{2,1,0:T(8,128)(2,1)S(1)}, bf16[4,16,1024]{2,1,0:T(8,128)(2,1)S(1)}, u32[]{:S(2)}, u32[]{:S(2)}) collective-permute-start(bf16[4,16,1024]{2,1,0:T(8,128)(2,1)S(1)} %collective-permute-done.5.refs_1_), channel_id=1, source_target_pairs={{0,1},{1,0},{2,3},{3,2},{4,5},{5,4},{6,7},{7,6},{8,9},{9,8},{10,11... | collective-permute-start | bytes 393224 | tf_op jit(solution)/shard_map/ppermute | solution.py:337
  17.4 0.0 collective-permute-done.1.refs_1_
  17.4 2.1 %collective-permute-done.2.refs_2_ = bf16[2,16,1024]{2,1,0:T(8,128)(2,1)S(1)} collective-permute-done((bf16[2,16,1024]{2,1,0:T(8,128)(2,1)S(1)}, bf16[2,16,1024]{2,1,0:T(8,128)(2,1)S(1)}, u32[]{:S(2)}, u32[]{:S(2)}) %collective-permute-start.2) | collective-permute-done | bytes 65568 | tf_op jit(solution)/shard_map/ppermute | solution.py:337
  19.4 2.6 %collective-permute-done.3.refs_3_ = bf16[2,16,1024]{2,1,0:T(8,128)(2,1)S(1)} collective-permute-done((bf16[2,16,1024]{2,1,0:T(8,128)(2,1)S(1)}, bf16[2,16,1024]{2,1,0:T(8,128)(2,1)S(1)}, u32[]{:S(2)}, u32[]{:S(2)}) %collective-permute-start.3) | collective-permute-done | bytes 65568 | tf_op jit(solution)/shard_map/ppermute | solution.py:337
  22.0 0.1 collective-permute-start.4
  22.1 0.3 shard_map.135
  22.4 0.8 %collective-permute-start.10 = (bf16[2,16,1024]{2,1,0:T(8,128)(2,1)S(1)}, bf16[2,16,1024]{2,1,0:T(8,128)(2,1)S(1)}, u32[]{:S(2)}, u32[]{:S(2)}) collective-permute-start(bf16[2,16,1024]{2,1,0:T(8,128)(2,1)S(1)} %get-tuple-element.63), channel_id=1, source_target_pairs={{0,6},{1,7},{2,4},{3,5},{4,2},{5,3},{6,0},{7,1},{8,14},{9,15},{10,... | collective-permute-start | bytes 196616 | tf_op jit(solution)/shard_map/ppermute | solution.py:337
  23.2 0.8 %collective-permute-start.8 = (bf16[2,16,1024]{2,1,0:T(8,128)(2,1)S(1)}, bf16[2,16,1024]{2,1,0:T(8,128)(2,1)S(1)}, u32[]{:S(2)}, u32[]{:S(2)}) collective-permute-start(bf16[2,16,1024]{2,1,0:T(8,128)(2,1)S(1)} %get-tuple-element.61), channel_id=1, source_target_pairs={{0,2},{1,3},{2,0},{3,1},{4,6},{5,7},{6,4},{7,5},{8,10},{9,11},{10,... | collective-permute-start | bytes 196616 | tf_op jit(solution)/shard_map/ppermute | solution.py:337
  24.0 1.9 %collective-permute-start.9 = (bf16[2,16,1024]{2,1,0:T(8,128)(2,1)S(1)}, bf16[2,16,1024]{2,1,0:T(8,128)(2,1)S(1)}, u32[]{:S(2)}, u32[]{:S(2)}) collective-permute-start(bf16[2,16,1024]{2,1,0:T(8,128)(2,1)S(1)} %get-tuple-element.62), channel_id=1, source_target_pairs={{0,4},{1,5},{2,6},{3,7},{4,0},{5,1},{6,2},{7,3},{8,12},{9,13},{10,... | collective-permute-start | bytes 196616 | tf_op jit(solution)/shard_map/ppermute | solution.py:337
  26.0 0.9 %shard_map.134 = (bf16[80,1024]{1,0:T(8,128)(2,1)}, bf16[256,80]{1,0:T(8,128)(2,1)S(1)}, f32[256,128]{1,0:T(8,128)S(1)}) custom-call(bf16[256,256]{1,0:T(8,128)(2,1)S(1)} %get-tuple-element.43.q, f32[256,128]{1,0:T(8,128)S(1)} %get-tuple-element.44.acc_old, f32[256,128]{1,0:T(8,128)S(1)} %get-tuple-element.45.max_old, ...), custom_call_target="tpu_custom_call" | custom-call | tf_op jit(solution)/shard_map/pallas_call | solution.py:341
  26.8 1.5 %collective-permute-done.10.refs_3_ = bf16[2,16,1024]{2,1,0:T(8,128)(2,1)S(1)} collective-permute-done((bf16[2,16,1024]{2,1,0:T(8,128)(2,1)S(1)}, bf16[2,16,1024]{2,1,0:T(8,128)(2,1)S(1)}, u32[]{:S(2)}, u32[]{:S(2)}) %collective-permute-start.10) | collective-permute-done | bytes 65568 | tf_op jit(solution)/shard_map/ppermute | solution.py:337
  28.3 0.5 %collective-permute-done.8.refs_1_ = bf16[2,16,1024]{2,1,0:T(8,128)(2,1)S(1)} collective-permute-done((bf16[2,16,1024]{2,1,0:T(8,128)(2,1)S(1)}, bf16[2,16,1024]{2,1,0:T(8,128)(2,1)S(1)}, u32[]{:S(2)}, u32[]{:S(2)}) %collective-permute-start.8) | collective-permute-done | bytes 65568 | tf_op jit(solution)/shard_map/ppermute | solution.py:337
  28.8 1.1 %shard_map.136 = (bf16[4,4,8192]{2,1,0:T(4,128)(2,1)}, bf16[80,1024]{1,0:T(8,128)(2,1)}) custom-call(bf16[4,4,8192]{2,1,0:T(4,128)(2,1)S(1)} %get-tuple-element.42.part_out, bf16[256,80]{1,0:T(8,128)(2,1)S(1)} %get-tuple-element.55.weights, f32[256,128]{1,0:T(8,128)S(1)} %get-tuple-element.56.base, bf16[5,8,16,128]{3,2,1,0:T(8,128)(2,1)S(1)} %get-tuple-element.47.land_mask, ...), custom_call_target="tpu_custom_call" | custom-call | tf_op jit(solution)/shard_map/pallas_call | solution.py:341
  (9 shorter events, 0.0 us)
Async XLA Ops:
  0.6 10.9 %collective-permute-start = (bf16[4,16,1024]{2,1,0:T(8,128)(2,1)}, bf16[4,16,1024]{2,1,0:T(8,128)(2,1)S(1)}, u32[]{:S(2)}, u32[]{:S(2)}) collective-permute-start(bf16[4,16,1024]{2,1,0:T(8,128)(2,1)} %bitcast.5), channel_id=1, source_target_pairs={{0,8},{1,9},{2,10},{3,11},{4,12},{5,13},{6,14},{7,15},{8,0},{9,1},... | collective-permute-start | bytes 393224 | tf_op jit(solution)/shard_map/ppermute | solution.py:337
  4.8 3.1 %copy-start.1 = (bf16[4,1,16,1024]{3,2,1,0:T(8,128)(2,1)S(1)}, bf16[4,1,16,1024]{3,2,1,0:T(8,128)(2,1)}, u32[]{:S(2)}) copy-start(bf16[4,1,16,1024]{3,2,1,0:T(8,128)(2,1)} %param.19) | copy-start | bytes 393220
  7.9 9.0 %collective-permute-start.5 = (bf16[4,16,1024]{2,1,0:T(8,128)(2,1)S(1)}, bf16[4,16,1024]{2,1,0:T(8,128)(2,1)S(1)}, u32[]{:S(2)}, u32[]{:S(2)}) collective-permute-start(bf16[4,16,1024]{2,1,0:T(8,128)(2,1)S(1)} %bitcast.7), channel_id=1, source_target_pairs={{0,8},{1,9},{2,10},{3,11},{4,12},{5,13},{6,14},{7,15},{8,0},{9,1},... | collective-permute-start | bytes 393224 | tf_op jit(solution)/shard_map/ppermute | solution.py:337
  8.0 3.6 %copy-start = (bf16[4,1,16,1024]{3,2,1,0:T(8,128)(2,1)S(1)}, bf16[4,1,16,1024]{3,2,1,0:T(8,128)(2,1)}, u32[]{:S(2)}) copy-start(bf16[4,1,16,1024]{3,2,1,0:T(8,128)(2,1)} %param.18) | copy-start | bytes 393220
  11.8 5.6 %collective-permute-start.1 = (bf16[2,16,1024]{2,1,0:T(8,128)(2,1)S(1)}, bf16[2,16,1024]{2,1,0:T(8,128)(2,1)S(1)}, u32[]{:S(2)}, u32[]{:S(2)}) collective-permute-start(bf16[2,16,1024]{2,1,0:T(8,128)(2,1)S(1)} %get-tuple-element.52), channel_id=1, source_target_pairs={{0,2},{1,3},{2,0},{3,1},{4,6},{5,7},{6,4},{7,5},{8,10},{9,11},{10,... | collective-permute-start | bytes 196616 | tf_op jit(solution)/shard_map/ppermute | solution.py:337
  13.5 5.9 %collective-permute-start.2 = (bf16[2,16,1024]{2,1,0:T(8,128)(2,1)S(1)}, bf16[2,16,1024]{2,1,0:T(8,128)(2,1)S(1)}, u32[]{:S(2)}, u32[]{:S(2)}) collective-permute-start(bf16[2,16,1024]{2,1,0:T(8,128)(2,1)S(1)} %get-tuple-element.53), channel_id=1, source_target_pairs={{0,4},{1,5},{2,6},{3,7},{4,0},{5,1},{6,2},{7,3},{8,12},{9,13},{10,... | collective-permute-start | bytes 196616 | tf_op jit(solution)/shard_map/ppermute | solution.py:337
  16.9 5.2 %collective-permute-start.3 = (bf16[2,16,1024]{2,1,0:T(8,128)(2,1)S(1)}, bf16[2,16,1024]{2,1,0:T(8,128)(2,1)S(1)}, u32[]{:S(2)}, u32[]{:S(2)}) collective-permute-start(bf16[2,16,1024]{2,1,0:T(8,128)(2,1)S(1)} %get-tuple-element.54), channel_id=1, source_target_pairs={{0,6},{1,7},{2,4},{3,5},{4,2},{5,3},{6,0},{7,1},{8,14},{9,15},{10,... | collective-permute-start | bytes 196616 | tf_op jit(solution)/shard_map/ppermute | solution.py:337
  16.9 5.3 %collective-permute-start.6 = (bf16[4,16,1024]{2,1,0:T(8,128)(2,1)S(1)}, bf16[4,16,1024]{2,1,0:T(8,128)(2,1)S(1)}, u32[]{:S(2)}, u32[]{:S(2)}) collective-permute-start(bf16[4,16,1024]{2,1,0:T(8,128)(2,1)S(1)} %bitcast.8), channel_id=1, source_target_pairs={{0,1},{1,0},{2,3},{3,2},{4,5},{5,4},{6,7},{7,6},{8,9},{9,8},{10,11... | collective-permute-start | bytes 393224 | tf_op jit(solution)/shard_map/ppermute | solution.py:337
  16.9 5.2 %collective-permute-start.7 = (bf16[4,16,1024]{2,1,0:T(8,128)(2,1)S(1)}, bf16[4,16,1024]{2,1,0:T(8,128)(2,1)S(1)}, u32[]{:S(2)}, u32[]{:S(2)}) collective-permute-start(bf16[4,16,1024]{2,1,0:T(8,128)(2,1)S(1)} %collective-permute-done.5.refs_1_), channel_id=1, source_target_pairs={{0,1},{1,0},{2,3},{3,2},{4,5},{5,4},{6,7},{7,6},{8,9},{9,8},{10,11... | collective-permute-start | bytes 393224 | tf_op jit(solution)/shard_map/ppermute | solution.py:337
  22.0 3.9 %collective-permute-start.4 = (bf16[4,16,1024]{2,1,0:T(8,128)(2,1)S(1)}, bf16[4,16,1024]{2,1,0:T(8,128)(2,1)S(1)}, u32[]{:S(2)}, u32[]{:S(2)}) collective-permute-start(bf16[4,16,1024]{2,1,0:T(8,128)(2,1)S(1)} %shard_map.133), channel_id=1, source_target_pairs={{0,1},{1,0},{2,3},{3,2},{4,5},{5,4},{6,7},{7,6},{8,9},{9,8},{10,11... | collective-permute-start | bytes 393224 | tf_op jit(solution)/shard_map/ppermute | solution.py:337
  22.4 5.9 %collective-permute-start.10 = (bf16[2,16,1024]{2,1,0:T(8,128)(2,1)S(1)}, bf16[2,16,1024]{2,1,0:T(8,128)(2,1)S(1)}, u32[]{:S(2)}, u32[]{:S(2)}) collective-permute-start(bf16[2,16,1024]{2,1,0:T(8,128)(2,1)S(1)} %get-tuple-element.63), channel_id=1, source_target_pairs={{0,6},{1,7},{2,4},{3,5},{4,2},{5,3},{6,0},{7,1},{8,14},{9,15},{10,... | collective-permute-start | bytes 196616 | tf_op jit(solution)/shard_map/ppermute | solution.py:337
  23.2 5.6 %collective-permute-start.8 = (bf16[2,16,1024]{2,1,0:T(8,128)(2,1)S(1)}, bf16[2,16,1024]{2,1,0:T(8,128)(2,1)S(1)}, u32[]{:S(2)}, u32[]{:S(2)}) collective-permute-start(bf16[2,16,1024]{2,1,0:T(8,128)(2,1)S(1)} %get-tuple-element.61), channel_id=1, source_target_pairs={{0,2},{1,3},{2,0},{3,1},{4,6},{5,7},{6,4},{7,5},{8,10},{9,11},{10,... | collective-permute-start | bytes 196616 | tf_op jit(solution)/shard_map/ppermute | solution.py:337
  24.0 4.8 %collective-permute-start.9 = (bf16[2,16,1024]{2,1,0:T(8,128)(2,1)S(1)}, bf16[2,16,1024]{2,1,0:T(8,128)(2,1)S(1)}, u32[]{:S(2)}, u32[]{:S(2)}) collective-permute-start(bf16[2,16,1024]{2,1,0:T(8,128)(2,1)S(1)} %get-tuple-element.62), channel_id=1, source_target_pairs={{0,4},{1,5},{2,6},{3,7},{4,0},{5,1},{6,2},{7,3},{8,12},{9,13},{10,... | collective-permute-start | bytes 196616 | tf_op jit(solution)/shard_map/ppermute | solution.py:337

commit v3 on v2

--- a/solution.py
+++ b/solution.py
@@ -226,11 +226,11 @@
                 out[s, :, pl.ds((g * SHARE + e) * HD, HD)] = tile.astype(jnp.bfloat16)
 
 
-def pick_kernel(laps, masks, pick_mask, *refs):
-    sources, outs = refs[: -len(masks)], refs[-len(masks) :]
+def pick_kernel(laps, places, pick_mask, *refs):
+    sources, outs = refs[: -len(places)], refs[-len(places) :]
     pairs = [sources[i : i + 2] for i in range(0, len(sources), 2)]
     width = sources[0].shape[2]
-    for i, out in enumerate(outs):
+    for i, out in zip(places, outs):
         for line in range(2):
             sides = pairs[line % len(pairs)]
             hits = [
@@ -412,19 +412,24 @@
     piece = jax.ShapeDtypeStruct((2, page_rows, width), bf16)
     small = pltpu.CompilerParams(vmem_limit_bytes=8 * 2**20)
 
-    def spread(*operands):
-        picked = kernel(
-            functools.partial(pick_kernel, laps, masks),
-            out_shape=(piece,) * len(masks),
+    def pick(places, *operands):
+        return kernel(
+            functools.partial(pick_kernel, laps, places),
+            out_shape=(piece,) * len(places),
             in_specs=[VMEM] * len(operands),
-            out_specs=(VMEM,) * len(masks),
+            out_specs=(VMEM,) * len(places),
             compiler_params=small,
         )(*operands)
+
+    def spread(picked):
         return [picked[0]] + [swap(x, mask) for x, mask in zip(picked[1:], masks[1:])]
 
     got_k, part_out = lax.optimization_barrier((got_k, part_out))
-    pieces_k = spread(mask_k, own_k, got_k)
-    pieces_v = spread(mask_v, own_v, got_v, twin_v, swap(got_v, 1))
+    every = tuple(range(len(masks)))
+    pieces_k = spread(pick(every, mask_k, own_k, got_k))
+    sources = (mask_v, own_v, got_v, twin_v, swap(got_v, 1))
+    (farthest,) = pick(every[-1:], *sources)
+    pieces_v = spread([*pick(every[:-1], *sources), farthest])
     joined = kernel(
         join_kernel,
         out_shape=jax.ShapeDtypeStruct((len(masks), page_rows, width), bf16),

time: 30.1 us -> 30.8 us (1.023)
  waiting for transfers between devices: 7.05 us -> 7.6 us
    ppermute x11, waiting for transfers between devices: 7.05 us -> 7.6 us  [swap(): return lax.ppermute(x, 'seq', [(i, i ^ mask) for i in range(chain)])]
    pallas_call x7 -> x8, Pallas kernels: 8.85 us -> 8.85 us  [call(): return pl.pallas_call(body, **settings)(*args)]
  transfers between devices with their start and end apart: 11 -> 11, of which waited for: 5 -> 5; matrix products, arithmetic and copies ran while one was open for 0% -> 0% of each run, Pallas kernels for 26% -> 25%
where the time goes in v3:
time: 30.8 us; the launch traced here: 30.6 us
  starting transfers between devices  13.4 us (44%)
  Pallas kernels  8.85 us (29%)
  waiting for transfers between devices  7.6 us (25%)
  between operations  0.71 us (2%)
    ppermute x11, starting transfers between devices, swap(): return lax.ppermute(x, 'seq', [(i, i ^ mask) for i in range(chain)])  13.4 us
    pallas_call x8, Pallas kernels, call(): return pl.pallas_call(body, **settings)(*args)  8.85 us
    ppermute x11, waiting for transfers between devices, swap(): return lax.ppermute(x, 'seq', [(i, i ^ mask) for i in range(chain)])  7.6 us
  transfers between devices with their start and end apart: 11, of which 5 were waited for; matrix products, arithmetic and copies ran while one was open for 0% of the time, Pallas kernels for 25%

profile of v3, /device:TPU:0, one launch (start us, length us, event | category | flops | bytes accessed | tf_op | source)
XLA Modules:
  0.0 30.6 jit_solution(12369712981256235127)
XLA Ops:
  0.6 4.1 %collective-permute-start = (bf16[4,16,1024]{2,1,0:T(8,128)(2,1)}, bf16[4,16,1024]{2,1,0:T(8,128)(2,1)S(1)}, u32[]{:S(2)}, u32[]{:S(2)}) collective-permute-start(bf16[4,16,1024]{2,1,0:T(8,128)(2,1)} %bitcast.9), channel_id=1, source_target_pairs={{0,8},{1,9},{2,10},{3,11},{4,12},{5,13},{6,14},{7,15},{8,0},{9,1},... | collective-permute-start | bytes 393224 | tf_op jit(solution)/shard_map/ppermute | solution.py:337
  4.8 3.1 %shard_map.130 = (f32[1024,128]{1,0:T(8,128)S(1)}, f32[2,128,128]{2,1,0:T(8,128)S(1)}, f32[1024,128]{1,0:T(8,128)S(1)}, bf16[64,16,1024]{2,1,0:T(8,128)(2,1)S(1)...) custom-call(s32[1]{0:T(128)} %bitcast.1.place, ...), custom_call_target="tpu_custom_call" | custom-call | tf_op jit(solution)/shard_map/pallas_call | solution.py:341
  7.9 0.1 collective-permute-start.5
  8.0 3.2 %shard_map.131 = (bf16[4,4,8192]{2,1,0:T(4,128)(2,1)S(1)}, bf16[256,256]{1,0:T(8,128)(2,1)S(1)}, f32[256,128]{1,0:T(8,128)S(1)}, f32[256,128]{1,0:T(8,128)S(1)}, f32[256,128]{1,0:T(8,128)S(1)}) custom-call(s32[1]{0:T(128)} %bitcast.1.place, s32[16]{0:T(128)} %turn_lengths_hbm.1, s32[16]{0:T(128)} %turn_slot_hbm.1, s32[4,16]{1,0:T(4,128)} %table_hbm.1, ...), custom_call_target="tpu_custom_call" | custom-call | flops 134217728 | bytes 4194304 | tf_op jit(solution)/shard_map/pallas_call | solution.py:341
  11.2 0.3 %collective-permute-done.refs_1_ = bf16[4,16,1024]{2,1,0:T(8,128)(2,1)S(1)} collective-permute-done((bf16[4,16,1024]{2,1,0:T(8,128)(2,1)}, bf16[4,16,1024]{2,1,0:T(8,128)(2,1)S(1)}, u32[]{:S(2)}, u32[]{:S(2)}) %collective-permute-start) | collective-permute-done | bytes 131104 | tf_op jit(solution)/shard_map/ppermute | solution.py:337
  11.6 0.3 shard_map.132
  11.8 1.7 %collective-permute-start.1 = (bf16[2,16,1024]{2,1,0:T(8,128)(2,1)S(1)}, bf16[2,16,1024]{2,1,0:T(8,128)(2,1)S(1)}, u32[]{:S(2)}, u32[]{:S(2)}) collective-permute-start(bf16[2,16,1024]{2,1,0:T(8,128)(2,1)S(1)} %get-tuple-element.51), channel_id=1, source_target_pairs={{0,2},{1,3},{2,0},{3,1},{4,6},{5,7},{6,4},{7,5},{8,10},{9,11},{10,... | collective-permute-start | bytes 196616 | tf_op jit(solution)/shard_map/ppermute | solution.py:337
  13.5 3.4 %collective-permute-start.2 = (bf16[2,16,1024]{2,1,0:T(8,128)(2,1)S(1)}, bf16[2,16,1024]{2,1,0:T(8,128)(2,1)S(1)}, u32[]{:S(2)}, u32[]{:S(2)}) collective-permute-start(bf16[2,16,1024]{2,1,0:T(8,128)(2,1)S(1)} %get-tuple-element.52), channel_id=1, source_target_pairs={{0,4},{1,5},{2,6},{3,7},{4,0},{5,1},{6,2},{7,3},{8,12},{9,13},{10,... | collective-permute-start | bytes 196616 | tf_op jit(solution)/shard_map/ppermute | solution.py:337
  16.9 0.0 collective-permute-start.3
  16.9 0.0 collective-permute-start.6
  16.9 0.0 collective-permute-done.5.refs_1_
  16.9 0.5 %collective-permute-start.7 = (bf16[4,16,1024]{2,1,0:T(8,128)(2,1)S(1)}, bf16[4,16,1024]{2,1,0:T(8,128)(2,1)S(1)}, u32[]{:S(2)}, u32[]{:S(2)}) collective-permute-start(bf16[4,16,1024]{2,1,0:T(8,128)(2,1)S(1)} %collective-permute-done.5.refs_1_), channel_id=1, source_target_pairs={{0,1},{1,0},{2,3},{3,2},{4,5},{5,4},{6,7},{7,6},{8,9},{9,8},{10,11... | collective-permute-start | bytes 393224 | tf_op jit(solution)/shard_map/ppermute | solution.py:337
  17.4 2.1 %collective-permute-done.2.refs_2_ = bf16[2,16,1024]{2,1,0:T(8,128)(2,1)S(1)} collective-permute-done((bf16[2,16,1024]{2,1,0:T(8,128)(2,1)S(1)}, bf16[2,16,1024]{2,1,0:T(8,128)(2,1)S(1)}, u32[]{:S(2)}, u32[]{:S(2)}) %collective-permute-start.2) | collective-permute-done | bytes 65568 | tf_op jit(solution)/shard_map/ppermute | solution.py:337
  19.4 2.6 %collective-permute-done.3.refs_3_ = bf16[2,16,1024]{2,1,0:T(8,128)(2,1)S(1)} collective-permute-done((bf16[2,16,1024]{2,1,0:T(8,128)(2,1)S(1)}, bf16[2,16,1024]{2,1,0:T(8,128)(2,1)S(1)}, u32[]{:S(2)}, u32[]{:S(2)}) %collective-permute-start.3) | collective-permute-done | bytes 65568 | tf_op jit(solution)/shard_map/ppermute | solution.py:337
  22.0 0.1 collective-permute-start.4
  22.1 0.2 shard_map.135
  22.3 0.6 %collective-permute-start.8 = (bf16[2,16,1024]{2,1,0:T(8,128)(2,1)S(1)}, bf16[2,16,1024]{2,1,0:T(8,128)(2,1)S(1)}, u32[]{:S(2)}, u32[]{:S(2)}) collective-permute-start(bf16[2,16,1024]{2,1,0:T(8,128)(2,1)S(1)} %get-tuple-element.60), channel_id=1, source_target_pairs={{0,2},{1,3},{2,0},{3,1},{4,6},{5,7},{6,4},{7,5},{8,10},{9,11},{10,... | collective-permute-start | bytes 196616 | tf_op jit(solution)/shard_map/ppermute | solution.py:337
  22.9 0.8 %collective-permute-start.9 = (bf16[2,16,1024]{2,1,0:T(8,128)(2,1)S(1)}, bf16[2,16,1024]{2,1,0:T(8,128)(2,1)S(1)}, u32[]{:S(2)}, u32[]{:S(2)}) collective-permute-start(bf16[2,16,1024]{2,1,0:T(8,128)(2,1)S(1)} %get-tuple-element.61), channel_id=1, source_target_pairs={{0,4},{1,5},{2,6},{3,7},{4,0},{5,1},{6,2},{7,3},{8,12},{9,13},{10,... | collective-permute-start | bytes 196616 | tf_op jit(solution)/shard_map/ppermute | solution.py:337
  23.7 0.1 shard_map.136
  23.8 2.2 %collective-permute-start.10 = (bf16[2,16,1024]{2,1,0:T(8,128)(2,1)S(1)}, bf16[2,16,1024]{2,1,0:T(8,128)(2,1)S(1)}, u32[]{:S(2)}, u32[]{:S(2)}) collective-permute-start(bf16[2,16,1024]{2,1,0:T(8,128)(2,1)S(1)} %shard_map.136), channel_id=1, source_target_pairs={{0,6},{1,7},{2,4},{3,5},{4,2},{5,3},{6,0},{7,1},{8,14},{9,15},{10,... | collective-permute-start | bytes 196616 | tf_op jit(solution)/shard_map/ppermute | solution.py:337
  26.0 0.9 %shard_map.134 = (bf16[80,1024]{1,0:T(8,128)(2,1)}, bf16[256,80]{1,0:T(8,128)(2,1)S(1)}, f32[256,128]{1,0:T(8,128)S(1)}) custom-call(bf16[256,256]{1,0:T(8,128)(2,1)S(1)} %get-tuple-element.42.q, f32[256,128]{1,0:T(8,128)S(1)} %get-tuple-element.43.acc_old, f32[256,128]{1,0:T(8,128)S(1)} %get-tuple-element.44.max_old, ...), custom_call_target="tpu_custom_call" | custom-call | tf_op jit(solution)/shard_map/pallas_call | solution.py:341
  26.9 0.6 %collective-permute-done.9.refs_2_ = bf16[2,16,1024]{2,1,0:T(8,128)(2,1)S(1)} collective-permute-done((bf16[2,16,1024]{2,1,0:T(8,128)(2,1)S(1)}, bf16[2,16,1024]{2,1,0:T(8,128)(2,1)S(1)}, u32[]{:S(2)}, u32[]{:S(2)}) %collective-permute-start.9) | collective-permute-done | bytes 65568 | tf_op jit(solution)/shard_map/ppermute | solution.py:337
  27.5 1.9 %collective-permute-done.10.refs_3_ = bf16[2,16,1024]{2,1,0:T(8,128)(2,1)S(1)} collective-permute-done((bf16[2,16,1024]{2,1,0:T(8,128)(2,1)S(1)}, bf16[2,16,1024]{2,1,0:T(8,128)(2,1)S(1)}, u32[]{:S(2)}, u32[]{:S(2)}) %collective-permute-start.10) | collective-permute-done | bytes 65568 | tf_op jit(solution)/shard_map/ppermute | solution.py:337
  29.5 1.1 %shard_map.137 = (bf16[4,4,8192]{2,1,0:T(4,128)(2,1)}, bf16[80,1024]{1,0:T(8,128)(2,1)}) custom-call(bf16[4,4,8192]{2,1,0:T(4,128)(2,1)S(1)} %get-tuple-element.41.part_out, bf16[256,80]{1,0:T(8,128)(2,1)S(1)} %get-tuple-element.54.weights, f32[256,128]{1,0:T(8,128)S(1)} %get-tuple-element.55.base, bf16[5,8,16,128]{3,2,1,0:T(8,128)(2,1)S(1)} %get-tuple-element.46.land_mask, ...), custom_call_target="tpu_custom_call" | custom-call | tf_op jit(solution)/shard_map/pallas_call | solution.py:341
  (10 shorter events, 0.0 us)
Async XLA Ops:
  0.6 10.9 %collective-permute-start = (bf16[4,16,1024]{2,1,0:T(8,128)(2,1)}, bf16[4,16,1024]{2,1,0:T(8,128)(2,1)S(1)}, u32[]{:S(2)}, u32[]{:S(2)}) collective-permute-start(bf16[4,16,1024]{2,1,0:T(8,128)(2,1)} %bitcast.9), channel_id=1, source_target_pairs={{0,8},{1,9},{2,10},{3,11},{4,12},{5,13},{6,14},{7,15},{8,0},{9,1},... | collective-permute-start | bytes 393224 | tf_op jit(solution)/shard_map/ppermute | solution.py:337
  4.8 3.1 %copy-start = (bf16[4,1,16,1024]{3,2,1,0:T(8,128)(2,1)S(1)}, bf16[4,1,16,1024]{3,2,1,0:T(8,128)(2,1)}, u32[]{:S(2)}) copy-start(bf16[4,1,16,1024]{3,2,1,0:T(8,128)(2,1)} %param.19) | copy-start | bytes 393220
  7.9 9.0 %collective-permute-start.5 = (bf16[4,16,1024]{2,1,0:T(8,128)(2,1)S(1)}, bf16[4,16,1024]{2,1,0:T(8,128)(2,1)S(1)}, u32[]{:S(2)}, u32[]{:S(2)}) collective-permute-start(bf16[4,16,1024]{2,1,0:T(8,128)(2,1)S(1)} %bitcast.5), channel_id=1, source_target_pairs={{0,8},{1,9},{2,10},{3,11},{4,12},{5,13},{6,14},{7,15},{8,0},{9,1},... | collective-permute-start | bytes 393224 | tf_op jit(solution)/shard_map/ppermute | solution.py:337
  8.0 3.6 %copy-start.1 = (bf16[4,1,16,1024]{3,2,1,0:T(8,128)(2,1)S(1)}, bf16[4,1,16,1024]{3,2,1,0:T(8,128)(2,1)}, u32[]{:S(2)}) copy-start(bf16[4,1,16,1024]{3,2,1,0:T(8,128)(2,1)} %param.18) | copy-start | bytes 393220
  11.8 5.6 %collective-permute-start.1 = (bf16[2,16,1024]{2,1,0:T(8,128)(2,1)S(1)}, bf16[2,16,1024]{2,1,0:T(8,128)(2,1)S(1)}, u32[]{:S(2)}, u32[]{:S(2)}) collective-permute-start(bf16[2,16,1024]{2,1,0:T(8,128)(2,1)S(1)} %get-tuple-element.51), channel_id=1, source_target_pairs={{0,2},{1,3},{2,0},{3,1},{4,6},{5,7},{6,4},{7,5},{8,10},{9,11},{10,... | collective-permute-start | bytes 196616 | tf_op jit(solution)/shard_map/ppermute | solution.py:337
  13.5 5.9 %collective-permute-start.2 = (bf16[2,16,1024]{2,1,0:T(8,128)(2,1)S(1)}, bf16[2,16,1024]{2,1,0:T(8,128)(2,1)S(1)}, u32[]{:S(2)}, u32[]{:S(2)}) collective-permute-start(bf16[2,16,1024]{2,1,0:T(8,128)(2,1)S(1)} %get-tuple-element.52), channel_id=1, source_target_pairs={{0,4},{1,5},{2,6},{3,7},{4,0},{5,1},{6,2},{7,3},{8,12},{9,13},{10,... | collective-permute-start | bytes 196616 | tf_op jit(solution)/shard_map/ppermute | solution.py:337
  16.9 5.2 %collective-permute-start.3 = (bf16[2,16,1024]{2,1,0:T(8,128)(2,1)S(1)}, bf16[2,16,1024]{2,1,0:T(8,128)(2,1)S(1)}, u32[]{:S(2)}, u32[]{:S(2)}) collective-permute-start(bf16[2,16,1024]{2,1,0:T(8,128)(2,1)S(1)} %get-tuple-element.53), channel_id=1, source_target_pairs={{0,6},{1,7},{2,4},{3,5},{4,2},{5,3},{6,0},{7,1},{8,14},{9,15},{10,... | collective-permute-start | bytes 196616 | tf_op jit(solution)/shard_map/ppermute | solution.py:337
  16.9 5.3 %collective-permute-start.6 = (bf16[4,16,1024]{2,1,0:T(8,128)(2,1)S(1)}, bf16[4,16,1024]{2,1,0:T(8,128)(2,1)S(1)}, u32[]{:S(2)}, u32[]{:S(2)}) collective-permute-start(bf16[4,16,1024]{2,1,0:T(8,128)(2,1)S(1)} %bitcast.6), channel_id=1, source_target_pairs={{0,1},{1,0},{2,3},{3,2},{4,5},{5,4},{6,7},{7,6},{8,9},{9,8},{10,11... | collective-permute-start | bytes 393224 | tf_op jit(solution)/shard_map/ppermute | solution.py:337
  16.9 5.2 %collective-permute-start.7 = (bf16[4,16,1024]{2,1,0:T(8,128)(2,1)S(1)}, bf16[4,16,1024]{2,1,0:T(8,128)(2,1)S(1)}, u32[]{:S(2)}, u32[]{:S(2)}) collective-permute-start(bf16[4,16,1024]{2,1,0:T(8,128)(2,1)S(1)} %collective-permute-done.5.refs_1_), channel_id=1, source_target_pairs={{0,1},{1,0},{2,3},{3,2},{4,5},{5,4},{6,7},{7,6},{8,9},{9,8},{10,11... | collective-permute-start | bytes 393224 | tf_op jit(solution)/shard_map/ppermute | solution.py:337
  22.0 4.0 %collective-permute-start.4 = (bf16[4,16,1024]{2,1,0:T(8,128)(2,1)S(1)}, bf16[4,16,1024]{2,1,0:T(8,128)(2,1)S(1)}, u32[]{:S(2)}, u32[]{:S(2)}) collective-permute-start(bf16[4,16,1024]{2,1,0:T(8,128)(2,1)S(1)} %shard_map.133), channel_id=1, source_target_pairs={{0,1},{1,0},{2,3},{3,2},{4,5},{5,4},{6,7},{7,6},{8,9},{9,8},{10,11... | collective-permute-start | bytes 393224 | tf_op jit(solution)/shard_map/ppermute | solution.py:337
  22.3 4.6 %collective-permute-start.8 = (bf16[2,16,1024]{2,1,0:T(8,128)(2,1)S(1)}, bf16[2,16,1024]{2,1,0:T(8,128)(2,1)S(1)}, u32[]{:S(2)}, u32[]{:S(2)}) collective-permute-start(bf16[2,16,1024]{2,1,0:T(8,128)(2,1)S(1)} %get-tuple-element.60), channel_id=1, source_target_pairs={{0,2},{1,3},{2,0},{3,1},{4,6},{5,7},{6,4},{7,5},{8,10},{9,11},{10,... | collective-permute-start | bytes 196616 | tf_op jit(solution)/shard_map/ppermute | solution.py:337
  22.9 4.6 %collective-permute-start.9 = (bf16[2,16,1024]{2,1,0:T(8,128)(2,1)S(1)}, bf16[2,16,1024]{2,1,0:T(8,128)(2,1)S(1)}, u32[]{:S(2)}, u32[]{:S(2)}) collective-permute-start(bf16[2,16,1024]{2,1,0:T(8,128)(2,1)S(1)} %get-tuple-element.61), channel_id=1, source_target_pairs={{0,4},{1,5},{2,6},{3,7},{4,0},{5,1},{6,2},{7,3},{8,12},{9,13},{10,... | collective-permute-start | bytes 196616 | tf_op jit(solution)/shard_map/ppermute | solution.py:337
  23.8 5.6 %collective-permute-start.10 = (bf16[2,16,1024]{2,1,0:T(8,128)(2,1)S(1)}, bf16[2,16,1024]{2,1,0:T(8,128)(2,1)S(1)}, u32[]{:S(2)}, u32[]{:S(2)}) collective-permute-start(bf16[2,16,1024]{2,1,0:T(8,128)(2,1)S(1)} %shard_map.136), channel_id=1, source_target_pairs={{0,6},{1,7},{2,4},{3,5},{4,2},{5,3},{6,0},{7,1},{8,14},{9,15},{10,... | collective-permute-start | bytes 196616 | tf_op jit(solution)/shard_map/ppermute | solution.py:337
